TPU v7x, 32 devices: a whole 2x2x4 slice. The times are simulated.
32 devices in a mesh: req: 2 (over y), patch: 16 (over z, x, core).
Axes of the slice: x: 2, y: 2, z: 4, core: 2. Of those that a mesh axis runs over, the one named last changes fastest.
Arguments:
- tokens: bfloat16 [1536, 1152], P(('req', 'patch')), parts along dimension 0, may hold values from -6 to 6
- positions: int32 [2, 1536], P(None, ('req', 'patch')), parts along dimension 1, may hold values from 0 to 95
- counts: int32 [32], P('req'), parts along dimension 0, may hold values from 1 to 48, 384 in all
- timestep: int32 [2], P('req'), parts along dimension 0, may hold values from 0 to 999
- time_in: bfloat16 [256, 1152], replicated, may hold values from -0.375 to 0.375
- time_out: bfloat16 [1152, 1152], P(None, 'patch'), may hold values from -0.1875 to 0.1875
- ada_weight: bfloat16 [1152, 3456], P('patch'), may hold values from -0.375 to 0.375
- qkv_weight: bfloat16 [1152, 3456], replicated, may hold values from -2 to 2, as said below
- out_weight: bfloat16 [1152, 1152], replicated, may hold values from -0.1875 to 0.1875
Outputs:
- block_out: bfloat16 [1536, 1152], P(('req', 'patch')), parts along dimension 0
There are 2 independent parts, one for each index of `req`. A program takes and returns all parts, laid end to end along the dimension named above; an argument that names none is the same for every part. Nothing has to cross between parts.
Inputs may be any that keep to these rules, and one draw needn't show every extreme that they name: `counts`: used slots are the first ones of each block; they sum to exactly 384, and some block uses all 48. `qkv_weight`: columns are 1152 of queries, 1152 of keys, 1152 of values, each head's 72 columns side by side.
All inputs are finite; a program needn't handle non-finite values.
Results may differ from a plain program's by a relative error of at most 0.0039.
Values may be sent and summed in bfloat16 or wider, within the bound.
No kernel may reach another device: no remote copies, remote signals or barrier semaphores. Data moves between devices by JAX's collectives and lax.ppermute only.
A program may use at most 64 MiB of HBM per device.

v0:
```python
import functools
import math

import jax
import jax.numpy as jnp
import numpy as np
from jax import lax
from jax.experimental import pallas as pl
from jax.experimental.pallas import tpu as pltpu
from jax.sharding import PartitionSpec as P


HEADS = 16
LANES = 128
SUM_ROWS = 8
CORE_MASK = 1
MERGE_MASK = 2
DIRECT_LIMIT = 16
neg_large = -1e30


def grant(mebibytes):
    return pltpu.CompilerParams(vmem_limit_bytes=mebibytes << 20)


def vmem():
    return pl.BlockSpec(memory_space=pltpu.VMEM)


def lane_table(model_width, freq_size):
    quarter = model_width // 4
    half = freq_size // 2
    lane = np.arange(model_width)
    table = np.zeros((SUM_ROWS, model_width), np.float32)
    table[0] = np.power(10000.0, -(lane % quarter) / quarter)
    table[1] = (lane // quarter) % 2
    table[2] = lane // (2 * quarter)
    feature = np.arange(freq_size)
    table[3, :freq_size] = np.exp(-math.log(10000.0) * (feature % half) / half)
    table[4, :freq_size] = feature < half
    return table


def sine(angle, shifted):
    turns = jnp.floor(angle * (0.5 / math.pi) + 0.5)
    rest = angle - turns * 6.28125
    rest = rest - turns * (2.0 * math.pi - 6.28125)
    rest = rest + shifted * (0.5 * math.pi)
    rest = jnp.where(rest > 0.5 * math.pi, math.pi - rest, rest)
    rest = jnp.where(rest < -0.5 * math.pi, -math.pi - rest, rest)
    square = rest * rest
    series = 1.0 / math.factorial(13)
    for power in (11, 9, 7, 5, 3, 1):
        sign = -1.0 if power % 4 == 3 else 1.0
        series = series * square + sign / math.factorial(power)
    return rest * series


def silu(value):
    return value / (1.0 + jnp.exp(-value))


def high_low(value):
    high = value.astype(jnp.bfloat16)
    return high, (value - high.astype(jnp.float32)).astype(jnp.bfloat16)


def front_kernel(
    part_index,
    parts,
    timestep,
    counts_far,
    tokens_far,
    positions_far,
    table_far,
    time_in_far,
    time_out_far,
    ada_weight_far,
    message,
    sums,
    x_in_ref,
    bias,
    row_valid,
    counts,
    tokens,
    positions,
    table,
    time_in,
    time_out,
    ada_weight,
    arrived,
):
    order = (
        (table_far, table),
        (time_in_far, time_in),
        (time_out_far, time_out),
        (ada_weight_far, ada_weight),
        (positions_far, positions),
        (tokens_far, tokens),
        (counts_far, counts),
    )
    copies = [
        pltpu.make_async_copy(far, near, arrived.at[index])
        for index, (far, near) in enumerate(order)
    ]
    for copy in copies:
        copy.start()
    rows, width = tokens.shape
    freq_size = time_in.shape[0]
    copies[0].wait()
    angle = timestep[0].astype(jnp.float32) * jnp.broadcast_to(
        table[3:4, :freq_size], (SUM_ROWS, freq_size)
    )
    shifted = jnp.broadcast_to(table[4:5, :freq_size], (SUM_ROWS, freq_size))
    features = sine(angle, shifted).astype(jnp.bfloat16)
    copies[1].wait()
    hidden = silu(jnp.dot(features, time_in[...], preferred_element_type=jnp.float32))
    copies[2].wait()
    cond = lax.dot_general(
        hidden.astype(jnp.bfloat16),
        time_out[...],
        (((1,), (1,)), ((), ())),
        preferred_element_type=jnp.float32,
    )
    copies[3].wait()
    partial = jnp.dot(
        silu(cond).astype(jnp.bfloat16), ada_weight[...], preferred_element_type=jnp.float32
    )
    row_id = lax.broadcasted_iota(jnp.int32, (SUM_ROWS, width), 0)
    packed = jnp.zeros((SUM_ROWS, width), jnp.float32)
    for piece in range(3):
        high, low = high_low(partial[:, piece * width : (piece + 1) * width])
        packed = jnp.where(row_id == 2 * piece, high.astype(jnp.float32), packed)
        packed = jnp.where(row_id == 2 * piece + 1, low.astype(jnp.float32), packed)
    packed = packed.astype(jnp.bfloat16)
    sums[...] = packed
    message[rows:, :] = packed

    copies[4].wait()
    place = positions[...].astype(jnp.float32)
    same = lax.broadcasted_iota(jnp.int32, (rows, rows), 0) == lax.broadcasted_iota(
        jnp.int32, (rows, rows), 1
    )
    column = [
        jnp.sum(jnp.where(same, place[axis : axis + 1, :], 0.0), axis=1, keepdims=True)
        for axis in range(2)
    ]
    where_to = jnp.where(table[2:3, :] > 0.5, column[1], column[0])
    embed = sine(where_to * table[0:1, :], table[1:2, :])
    copies[5].wait()
    x_in = tokens[...].astype(jnp.float32) + embed
    x_in_ref[...] = x_in
    centered = x_in - jnp.mean(x_in, axis=1, keepdims=True)
    variance = jnp.mean(centered * centered, axis=1, keepdims=True)
    message[:rows, :] = (centered * lax.rsqrt(variance + 1e-06)).astype(jnp.bfloat16)

    copies[6].wait()
    my_index = lax.axis_index("patch")
    key_id = lax.broadcasted_iota(jnp.int32, bias.shape, 1)
    valid = key_id < 0
    for block in range(parts):
        first = block * rows
        used = counts[part_index(my_index, block)]
        valid = jnp.logical_or(valid, jnp.logical_and(key_id >= first, key_id < first + used))
    bias[...] = jnp.where(valid, 0.0, neg_large)
    own_row = lax.broadcasted_iota(jnp.int32, row_valid.shape, 0)
    row_valid[...] = (own_row < counts[my_index]).astype(jnp.float32)


def load_kernel(after, weight_far, weight, arrived):
    pieces = arrived.shape[0]
    size = weight.shape[0] // pieces
    copies = [
        pltpu.make_async_copy(
            weight_far.at[pl.ds(index * size, size)],
            weight.at[pl.ds(index * size, size)],
            arrived.at[index],
        )
        for index in range(pieces)
    ]
    for copy in copies:
        copy.start()
    for copy in copies:
        copy.wait()


def unpack_sums(packed):
    width = packed.shape[1]
    value = packed.astype(jnp.float32)
    row_id = lax.broadcasted_iota(jnp.int32, (SUM_ROWS, width), 0)
    out = jnp.zeros((SUM_ROWS, width), jnp.float32)
    for piece in range(3):
        both = value[2 * piece : 2 * piece + 1, :] + value[2 * piece + 1 : 2 * piece + 2, :]
        out = jnp.where(row_id == piece, both, out)
    return out


def add_kernel(*refs):
    out = refs[-1]
    total = None
    for ref in refs[:-1]:
        rows = ref.shape[0]
        value = ref[rows - SUM_ROWS :, :].astype(jnp.float32)
        total = value if total is None else total + value
    out[...] = unpack_sums(total)


def attend_kernel(block_rows, key_count, *refs):
    bias, sums_a, sums_b = refs[:3]
    key_refs = refs[3 : 3 + key_count]
    query_refs = refs[3 + key_count : 7 + key_count]
    weight = refs[7 + key_count]
    near_out, far_out = refs[8 + key_count : 10 + key_count]
    mod_keys, mod_queries, keys, values, queries = refs[10 + key_count :]
    width = weight.shape[0]
    head_size = width // HEADS
    sums = sums_a[...] + sums_b[...]
    shift = sums[0:1, :]
    scale = 1.0 + sums[1:2, :]

    def modulate(value):
        return (value.astype(jnp.float32) * scale + shift).astype(jnp.bfloat16)

    place = 0
    for ref in key_refs:
        for start in range(0, ref.shape[0], block_rows + SUM_ROWS):
            mod_keys[place : place + block_rows, :] = modulate(ref[start : start + block_rows, :])
            place += block_rows
    for index, ref in enumerate(query_refs):
        mod_queries[index * block_rows : (index + 1) * block_rows, :] = modulate(
            ref[:block_rows, :]
        )
    piece = 3 * LANES
    for start in range(0, width, piece):
        stop = min(start + piece, width)
        queries[:, start:stop] = jnp.dot(
            mod_queries[...], weight[:, start:stop], preferred_element_type=jnp.float32
        ).astype(jnp.bfloat16)
        keys[:, start:stop] = jnp.dot(
            mod_keys[...], weight[:, width + start : width + stop], preferred_element_type=jnp.float32
        ).astype(jnp.bfloat16)
        values[:, start:stop] = jnp.dot(
            mod_keys[...],
            weight[:, 2 * width + start : 2 * width + stop],
            preferred_element_type=jnp.float32,
        ).astype(jnp.bfloat16)

    total_queries = queries.shape[0]
    half = total_queries // 2
    base_two = math.log2(math.e) / math.sqrt(head_size)
    lse_lane = lax.broadcasted_iota(jnp.int32, (total_queries, LANES), 1)
    lse_all = jnp.zeros((total_queries, LANES), jnp.float32)
    key_bias = bias[0:1, :]
    held = None
    for head in range(HEADS):
        low, high = head * head_size, (head + 1) * head_size
        first, last = low // LANES * LANES, -(-high // LANES) * LANES
        lane = lax.broadcasted_iota(jnp.int32, (1, last - first), 1) + first
        inside = jnp.logical_and(lane >= low, lane < high)
        query = jnp.where(inside, queries[:, first:last], jnp.zeros((), jnp.bfloat16))
        scores = lax.dot_general(
            query,
            keys[:, first:last],
            (((1,), (1,)), ((), ())),
            preferred_element_type=jnp.float32,
        )
        scores = scores + key_bias
        top = jnp.max(scores, axis=1, keepdims=True)
        weights = jnp.exp2((scores - top) * base_two)
        total = jnp.sum(weights, axis=1, keepdims=True)
        result = jnp.dot(
            weights.astype(jnp.bfloat16), values[:, first:last], preferred_element_type=jnp.float32
        )
        result = result * (1.0 / total)
        lse_all = jnp.where(lse_lane == head, top * base_two + jnp.log2(total), lse_all)
        for start in range(first, last, LANES):
            tile = result[:, start - first : start - first + LANES]
            if start < low:
                tile = jnp.where(inside[:, start - first : start - first + LANES], tile, held)
            if start + LANES <= high:
                tile = tile.astype(jnp.bfloat16)
                near_out[:, start : start + LANES] = tile[:half, :]
                far_out[:, start : start + LANES] = tile[half:, :]
            else:
                held = tile
    packed = pack_lse(lse_all)
    near_out[:, width:] = packed[:half, :]
    far_out[:, width:] = packed[half:, :]


def pack_lse(lse):
    high = lse.astype(jnp.bfloat16).astype(jnp.float32)
    middle = (lse - high).astype(jnp.bfloat16).astype(jnp.float32)
    low = lse - high - middle
    return (high + pltpu.roll(middle, HEADS, 1) + pltpu.roll(low, 2 * HEADS, 1)).astype(
        jnp.bfloat16
    )


def unpack_lse(packed):
    source = lax.broadcasted_iota(jnp.int32, (LANES, LANES), 0)
    target = lax.broadcasted_iota(jnp.int32, (LANES, LANES), 1)
    chosen = source == target
    for piece in range(1, 3):
        chosen = jnp.logical_or(chosen, source == target + piece * HEADS)
    chosen = jnp.logical_and(chosen, target < HEADS).astype(jnp.bfloat16)
    return jnp.dot(packed, chosen, preferred_element_type=jnp.float32)


def spread(value, width):
    head_size = width // HEADS
    head_id = lax.broadcasted_iota(jnp.int32, (LANES, width), 0)
    lane_id = lax.broadcasted_iota(jnp.int32, (LANES, width), 1)
    low = head_id * head_size
    expand = jnp.logical_and(lane_id >= low, lane_id < low + head_size).astype(jnp.bfloat16)
    high, rest = high_low(value)
    return jnp.dot(high, expand, preferred_element_type=jnp.float32) + jnp.dot(
        rest, expand, preferred_element_type=jnp.float32
    )


def merge(packed_a, packed_b):
    width = packed_a.shape[1] - LANES
    lse_a, lse_b = unpack_lse(packed_a[:, width:]), unpack_lse(packed_b[:, width:])
    top = jnp.maximum(lse_a, lse_b)
    part_a = jnp.exp2(lse_a - top)
    part_b = jnp.exp2(lse_b - top)
    total = part_a + part_b
    share = spread(part_b / total, width)
    first = packed_a[:, :width].astype(jnp.float32)
    value = first + share * (packed_b[:, :width].astype(jnp.float32) - first)
    return value, top + jnp.log2(total)


def merge_kernel(packed_a, packed_b, own_out, send_out):
    value, lse = merge(packed_a[...], packed_b[...])
    rows, width = own_out.shape[0], value.shape[1]
    value = value.astype(jnp.bfloat16)
    lane = lax.broadcasted_iota(jnp.int32, lse.shape, 1)
    packed = pack_lse(jnp.where(lane < HEADS, lse, 0.0))
    own_out[:, :width] = value[:rows, :]
    own_out[:, width:] = packed[:rows, :]
    send_out[:, :width] = value[rows:, :]
    send_out[:, width:] = packed[rows:, :]


def finish_kernel(packed_a, packed_b, x_in, row_valid, sums_a, sums_b, weight, out):
    value, _ = merge(packed_a[...], packed_b[...])
    gate = sums_a[2:3, :] + sums_b[2:3, :]
    projected = jnp.dot(
        value.astype(jnp.bfloat16), weight[...], preferred_element_type=jnp.float32
    )
    out[...] = (x_in[...] + gate * projected * row_valid[:, 0:1]).astype(jnp.bfloat16)


def far():
    return pl.BlockSpec(memory_space=pltpu.HBM)


def stay_far(array):
    return pltpu.with_memory_space_constraint(array, pltpu.HBM)


def per_device(
    tokens, positions, counts, timestep, time_in, time_out, ada_weight, qkv_weight, out_weight
):
    devices = lax.axis_size("patch")
    rows, width = tokens.shape
    shape = jax.ShapeDtypeStruct
    table = jnp.asarray(lane_table(width, time_in.shape[0]))
    key_masks = [mask for mask in range(devices) if not mask & (CORE_MASK | MERGE_MASK)]
    direct = devices <= DIRECT_LIMIT

    def swap(value, mask):
        pairs = [(index, index ^ mask) for index in range(devices)]
        return lax.ppermute(value, "patch", pairs)

    def part_index(my_index, block):
        if direct:
            return jnp.bitwise_xor(my_index, key_masks[block])
        return jnp.bitwise_and(my_index, CORE_MASK | MERGE_MASK) + key_masks[block]

    inputs = (timestep, counts, tokens, positions, table, time_in, time_out.T, ada_weight)
    message, sums, x_in, bias, row_valid = pl.pallas_call(
        functools.partial(front_kernel, part_index, len(key_masks)),
        out_shape=(
            shape((rows + SUM_ROWS, width), jnp.bfloat16),
            shape((SUM_ROWS, width), jnp.bfloat16),
            shape((rows, width), jnp.float32),
            shape((SUM_ROWS, rows * len(key_masks)), jnp.float32),
            shape((rows, LANES), jnp.float32),
        ),
        in_specs=[pl.BlockSpec(memory_space=pltpu.SMEM)] + [far()] * (len(inputs) - 1),
        out_specs=(vmem(),) * 5,
        scratch_shapes=[
            (pltpu.SMEM if array.ndim == 1 else pltpu.VMEM)(array.shape, array.dtype)
            for array in inputs[1:]
        ]
        + [pltpu.SemaphoreType.DMA((len(inputs) - 1,))],
        compiler_params=grant(8),
        name="front",
    )(inputs[0], *[stay_far(array) for array in inputs[1:]])

    load = pl.pallas_call(
        load_kernel,
        out_shape=shape(qkv_weight.shape, qkv_weight.dtype),
        in_specs=[vmem(), far()],
        out_specs=vmem(),
        scratch_shapes=[pltpu.SemaphoreType.DMA((8,))],
        compiler_params=grant(1),
        cost_estimate=pl.CostEstimate(
            flops=1 << 32, bytes_accessed=4 * qkv_weight.size, transcendentals=0
        ),
        name="load",
    )
    weight = load(row_valid, stay_far(qkv_weight))

    if direct:
        got = {mask: swap(message, mask) for mask in [*key_masks[1:], MERGE_MASK]}
        others = [mask | MERGE_MASK for mask in key_masks[1:]]
        got_sums = [swap(sums, mask) for mask in others]
        key_parts = [message] + [got[mask] for mask in key_masks[1:]]
        across = got[MERGE_MASK]
        addends = (sums, *got.values(), *got_sums)
    else:
        across = swap(message, MERGE_MASK)
        spread_mask = CORE_MASK | MERGE_MASK
        groups = [[mask | rest for mask in key_masks] for rest in range(spread_mask + 1)]
        key_parts = [lax.all_gather(message, "patch", axis_index_groups=groups, tiled=True)]
        running = sums.astype(jnp.float32)
        step = MERGE_MASK
        while step < devices:
            running = running + swap(running, step)
            step *= 2
        addends = (running,)
    half_sums = pl.pallas_call(
        add_kernel,
        out_shape=shape((SUM_ROWS, width), jnp.float32),
        in_specs=[vmem()] * len(addends),
        out_specs=vmem(),
        compiler_params=grant(4),
        name="add",
    )(*addends)
    other_sums = swap(half_sums, CORE_MASK)
    other_own = swap(message, CORE_MASK)
    other_across = swap(across, CORE_MASK)

    total_keys = rows * len(key_masks)
    total_queries = 4 * rows
    half = total_queries // 2
    near, away = pl.pallas_call(
        functools.partial(attend_kernel, rows, len(key_parts)),
        out_shape=(shape((half, width + LANES), jnp.bfloat16),) * 2,
        in_specs=[vmem()] * (8 + len(key_parts)),
        out_specs=(vmem(),) * 2,
        scratch_shapes=[
            pltpu.VMEM((total_keys, width), jnp.bfloat16),
            pltpu.VMEM((total_queries, width), jnp.bfloat16),
            pltpu.VMEM((total_keys, width), jnp.bfloat16),
            pltpu.VMEM((total_keys, width), jnp.bfloat16),
            pltpu.VMEM((total_queries, width), jnp.bfloat16),
        ],
        compiler_params=grant(32),
        name="attend",
    )(
        bias,
        half_sums,
        other_sums,
        *key_parts,
        message,
        across,
        other_own,
        other_across,
        weight,
    )
    own, send = pl.pallas_call(
        merge_kernel,
        out_shape=(shape((rows, width + LANES), jnp.bfloat16),) * 2,
        in_specs=[vmem()] * 2,
        out_specs=(vmem(),) * 2,
        compiler_params=grant(6),
        name="merge",
    )(near, swap(away, CORE_MASK))
    return pl.pallas_call(
        finish_kernel,
        out_shape=shape((rows, width), jnp.bfloat16),
        in_specs=[vmem()] * 7,
        out_specs=vmem(),
        compiler_params=grant(8),
        name="finish",
    )(own, swap(send, MERGE_MASK), x_in, row_valid, half_sums, other_sums, out_weight)


def solution(mesh):
    placed = (
        P(("req", "patch"), None),
        P(None, ("req", "patch")),
        P("req"),
        P("req"),
        P(),
        P(None, "patch"),
        P("patch", None),
        P(),
        P(),
    )

    return jax.shard_map(
        per_device, mesh=mesh, in_specs=placed, out_specs=P(("req", "patch"), None), check_vma=False
    )
```

profile of v0, /device:TPU:0, one launch (start us, length us, event | category | flops | bytes accessed | tf_op | source)
XLA Modules:
  0.0 47.8 jit_solution(1619265375388669413)
XLA Ops:
  0.7 2.4 %front.1 = (bf16[56,1152]{1,0:T(8,128)(2,1)S(1)}, bf16[8,1152]{1,0:T(8,128)(2,1)S(1)}, f32[48,1152]{1,0:T(8,128)S(1)}, f32[8,192]{1,0:T(8,128)S(1)}, f32[48,128]{1,0:T(8,128)S(1)}) custom-call(s32[1]{0:T(128)S(6)} %copy.11.timestep, s32[16]{0:T(128)} %counts_far.1, bf16[48,1152]{1,0:T(8,128)(2,1)} %tokens_far.1, s32[2,48]{1,0:T(2,128)} %positions_far.1, ...), custom_call_target="tpu_custom_call" | custom-call | tf_op jit(solution)/shard_map/front/pallas_call | solution.py:384
  3.1 3.0 %collective-permute-start.3 = (bf16[56,1152]{1,0:T(8,128)(2,1)S(1)}, bf16[56,1152]{1,0:T(8,128)(2,1)S(1)}, u32[]{:S(2)}, u32[]{:S(2)}) collective-permute-start(bf16[56,1152]{1,0:T(8,128)(2,1)S(1)} %get-tuple-element.16.refs_3_.refs_7_), channel_id=1, source_target_pairs={{0,2},{1,3},{2,0},{3,1},{4,6},{5,7},{6,4},{7,5},{8,10},{9,11},{10,... | collective-permute-start | bytes 387080 | tf_op jit(solution)/shard_map/ppermute | solution.py:376
  6.1 3.6 %collective-permute-start.2 = (bf16[56,1152]{1,0:T(8,128)(2,1)S(1)}, bf16[56,1152]{1,0:T(8,128)(2,1)S(1)}, u32[]{:S(2)}, u32[]{:S(2)}) collective-permute-start(bf16[56,1152]{1,0:T(8,128)(2,1)S(1)} %get-tuple-element.16.refs_3_.refs_7_), channel_id=1, source_target_pairs={{0,12},{1,13},{2,14},{3,15},{4,8},{5,9},{6,10},{7,11},{8,4},{9,5},... | collective-permute-start | bytes 387080 | tf_op jit(solution)/shard_map/ppermute | solution.py:376
  9.7 0.0 collective-permute-start.1
  9.7 0.8 %collective-permute-start = (bf16[56,1152]{1,0:T(8,128)(2,1)S(1)}, bf16[56,1152]{1,0:T(8,128)(2,1)S(1)}, u32[]{:S(2)}, u32[]{:S(2)}) collective-permute-start(bf16[56,1152]{1,0:T(8,128)(2,1)S(1)} %get-tuple-element.16.refs_3_.refs_7_), channel_id=1, source_target_pairs={{0,4},{1,5},{2,6},{3,7},{4,0},{5,1},{6,2},{7,3},{8,12},{9,13},{10,... | collective-permute-start | bytes 387080 | tf_op jit(solution)/shard_map/ppermute | solution.py:376
  10.5 3.6 %collective-permute-start.6 = (bf16[8,1152]{1,0:T(8,128)(2,1)S(1)}, bf16[8,1152]{1,0:T(8,128)(2,1)S(1)}, u32[]{:S(2)}, u32[]{:S(2)}) collective-permute-start(bf16[8,1152]{1,0:T(8,128)(2,1)S(1)} %get-tuple-element.15.refs_0_), channel_id=1, source_target_pairs={{0,14},{1,15},{2,12},{3,13},{4,10},{5,11},{6,8},{7,9},{8,6},{9,7},... | collective-permute-start | bytes 55304 | tf_op jit(solution)/shard_map/ppermute | solution.py:376
  14.1 4.9 %collective-permute-done.6.refs_7_ = bf16[8,1152]{1,0:T(8,128)(2,1)S(1)} collective-permute-done((bf16[8,1152]{1,0:T(8,128)(2,1)S(1)}, bf16[8,1152]{1,0:T(8,128)(2,1)S(1)}, u32[]{:S(2)}, u32[]{:S(2)}) %collective-permute-start.6) | collective-permute-done | bytes 18464 | tf_op jit(solution)/shard_map/ppermute | solution.py:376
  18.9 4.7 %collective-permute-start.5 = (bf16[8,1152]{1,0:T(8,128)(2,1)S(1)}, bf16[8,1152]{1,0:T(8,128)(2,1)S(1)}, u32[]{:S(2)}, u32[]{:S(2)}) collective-permute-start(bf16[8,1152]{1,0:T(8,128)(2,1)S(1)} %get-tuple-element.15.refs_0_), channel_id=1, source_target_pairs={{0,10},{1,11},{2,8},{3,9},{4,14},{5,15},{6,12},{7,13},{8,2},{9,3},... | collective-permute-start | bytes 55304 | tf_op jit(solution)/shard_map/ppermute | solution.py:376
  23.6 1.7 %collective-permute-done.5.refs_6_ = bf16[8,1152]{1,0:T(8,128)(2,1)S(1)} collective-permute-done((bf16[8,1152]{1,0:T(8,128)(2,1)S(1)}, bf16[8,1152]{1,0:T(8,128)(2,1)S(1)}, u32[]{:S(2)}, u32[]{:S(2)}) %collective-permute-start.5) | collective-permute-done | bytes 18464 | tf_op jit(solution)/shard_map/ppermute | solution.py:376
  25.3 2.8 %collective-permute-start.4 = (bf16[8,1152]{1,0:T(8,128)(2,1)S(1)}, bf16[8,1152]{1,0:T(8,128)(2,1)S(1)}, u32[]{:S(2)}, u32[]{:S(2)}) collective-permute-start(bf16[8,1152]{1,0:T(8,128)(2,1)S(1)} %get-tuple-element.15.refs_0_), channel_id=1, source_target_pairs={{0,6},{1,7},{2,4},{3,5},{4,2},{5,3},{6,0},{7,1},{8,14},{9,15},{10,... | collective-permute-start | bytes 55304 | tf_op jit(solution)/shard_map/ppermute | solution.py:376
  28.2 1.9 %collective-permute-done.4.refs_5_ = bf16[8,1152]{1,0:T(8,128)(2,1)S(1)} collective-permute-done((bf16[8,1152]{1,0:T(8,128)(2,1)S(1)}, bf16[8,1152]{1,0:T(8,128)(2,1)S(1)}, u32[]{:S(2)}, u32[]{:S(2)}) %collective-permute-start.4) | collective-permute-done | bytes 18464 | tf_op jit(solution)/shard_map/ppermute | solution.py:376
  30.0 0.0 collective-permute-start.8
  30.0 0.0 collective-permute-done.3.refs_4_.refs_8_
  30.0 0.0 collective-permute-done.2.refs_3_.refs_6_
  30.0 0.0 collective-permute-done.1.refs_2_.refs_5_
  30.0 0.0 collective-permute-done.refs_1_.refs_4_
  30.1 0.6 %collective-permute-start.7 = (f32[8,1152]{1,0:T(8,128)S(1)}, f32[8,1152]{1,0:T(8,128)S(1)}, u32[]{:S(2)}, u32[]{:S(2)}) collective-permute-start(f32[8,1152]{1,0:T(8,128)S(1)} %add.1.refs_1_.sums_a), channel_id=1, source_target_pairs={{0,1},{1,0},{2,3},{3,2},{4,5},{5,4},{6,7},{7,6},{8,9},{9,8},{10,11... | collective-permute-start | bytes 110600 | tf_op jit(solution)/shard_map/ppermute | solution.py:376
  30.7 0.1 collective-permute-start.9
  30.7 3.3 %load.1.refs_11_ = bf16[1152,3456]{1,0:T(8,128)(2,1)S(1)} custom-call(f32[48,128]{1,0:T(8,128)S(1)} %get-tuple-element.17.after.row_valid, bf16[1152,3456]{1,0:T(8,128)(2,1)} %weight_far.1), custom_call_target="tpu_custom_call" | custom-call | flops 4294967296 | bytes 15925248 | tf_op jit(solution)/shard_map/load/pallas_call | solution.py:416
  34.1 0.0 copy-start
  34.1 0.0 collective-permute-done.8.refs_9_
  34.1 0.0 collective-permute-done.7.refs_2_.sums_b
  34.1 0.0 collective-permute-done.9.refs_10_
  34.1 4.3 %attend.1 = (bf16[96,1280]{1,0:T(8,128)(2,1)S(1)}, bf16[96,1280]{1,0:T(8,128)(2,1)S(1)}) custom-call(f32[8,192]{1,0:T(8,128)S(1)} %get-tuple-element.14.refs_0_, f32[8,1152]{1,0:T(8,128)S(1)} %add.1.refs_1_.sums_a, f32[8,1152]{1,0:T(8,128)S(1)} %collective-permute-done.7.refs_2_.sums_b, bf16[56,1152]{1,0:T(8,128)(2,1)S(1)} %get-tuple-element.16.refs_3_.refs_7_, ...), custom_call_target="tpu_custom_call" | custom-call | tf_op jit(solution)/shard_map/attend/pallas_call | solution.py:451
  38.4 0.5 %collective-permute-start.10 = (bf16[96,1280]{1,0:T(8,128)(2,1)S(1)}, bf16[96,1280]{1,0:T(8,128)(2,1)S(1)}, u32[]{:S(2)}, u32[]{:S(2)}) collective-permute-start(bf16[96,1280]{1,0:T(8,128)(2,1)S(1)} %get-tuple-element.19), channel_id=1, source_target_pairs={{0,1},{1,0},{2,3},{3,2},{4,5},{5,4},{6,7},{7,6},{8,9},{9,8},{10,11... | collective-permute-start | bytes 737288 | tf_op jit(solution)/shard_map/ppermute | solution.py:376
  38.9 1.1 %collective-permute-done.10.packed_b = bf16[96,1280]{1,0:T(8,128)(2,1)S(1)} collective-permute-done((bf16[96,1280]{1,0:T(8,128)(2,1)S(1)}, bf16[96,1280]{1,0:T(8,128)(2,1)S(1)}, u32[]{:S(2)}, u32[]{:S(2)}) %collective-permute-start.10) | collective-permute-done | bytes 245792 | tf_op jit(solution)/shard_map/ppermute | solution.py:376
  40.0 0.5 %merge.1 = (bf16[48,1280]{1,0:T(8,128)(2,1)S(1)}, bf16[48,1280]{1,0:T(8,128)(2,1)S(1)}) custom-call(bf16[96,1280]{1,0:T(8,128)(2,1)S(1)} %get-tuple-element.18.packed_a, bf16[96,1280]{1,0:T(8,128)(2,1)S(1)} %collective-permute-done.10.packed_b), custom_call_target="tpu_custom_call" | custom-call | tf_op jit(solution)/shard_map/merge/pallas_call | solution.py:476
  40.5 0.9 %collective-permute-start.11 = (bf16[48,1280]{1,0:T(8,128)(2,1)S(1)}, bf16[48,1280]{1,0:T(8,128)(2,1)S(1)}, u32[]{:S(2)}, u32[]{:S(2)}) collective-permute-start(bf16[48,1280]{1,0:T(8,128)(2,1)S(1)} %get-tuple-element.21), channel_id=1, source_target_pairs={{0,2},{1,3},{2,0},{3,1},{4,6},{5,7},{6,4},{7,5},{8,10},{9,11},{10,... | collective-permute-start | bytes 368648 | tf_op jit(solution)/shard_map/ppermute | solution.py:376
  41.4 4.8 %collective-permute-done.11.packed_b = bf16[48,1280]{1,0:T(8,128)(2,1)S(1)} collective-permute-done((bf16[48,1280]{1,0:T(8,128)(2,1)S(1)}, bf16[48,1280]{1,0:T(8,128)(2,1)S(1)}, u32[]{:S(2)}, u32[]{:S(2)}) %collective-permute-start.11) | collective-permute-done | bytes 122912 | tf_op jit(solution)/shard_map/ppermute | solution.py:376
  46.2 0.0 copy-done
  46.2 1.6 %finish.1 = bf16[48,1152]{1,0:T(8,128)(2,1)} custom-call(bf16[48,1280]{1,0:T(8,128)(2,1)S(1)} %get-tuple-element.20.packed_a, bf16[48,1280]{1,0:T(8,128)(2,1)S(1)} %collective-permute-done.11.packed_b, f32[48,1152]{1,0:T(8,128)S(1)} %get-tuple-element.22.x_in, f32[48,128]{1,0:T(8,128)S(1)} %get-tuple-element.17.after.row_valid, ...), custom_call_target="tpu_custom_call" | custom-call | tf_op jit(solution)/shard_map/finish/pallas_call | solution.py:484
  (1 shorter events, 0.0 us)
Async XLA Ops:
  3.1 26.9 %collective-permute-start.3 = (bf16[56,1152]{1,0:T(8,128)(2,1)S(1)}, bf16[56,1152]{1,0:T(8,128)(2,1)S(1)}, u32[]{:S(2)}, u32[]{:S(2)}) collective-permute-start(bf16[56,1152]{1,0:T(8,128)(2,1)S(1)} %get-tuple-element.16.refs_3_.refs_7_), channel_id=1, source_target_pairs={{0,2},{1,3},{2,0},{3,1},{4,6},{5,7},{6,4},{7,5},{8,10},{9,11},{10,... | collective-permute-start | bytes 387080 | tf_op jit(solution)/shard_map/ppermute | solution.py:376
  6.1 23.9 %collective-permute-start.2 = (bf16[56,1152]{1,0:T(8,128)(2,1)S(1)}, bf16[56,1152]{1,0:T(8,128)(2,1)S(1)}, u32[]{:S(2)}, u32[]{:S(2)}) collective-permute-start(bf16[56,1152]{1,0:T(8,128)(2,1)S(1)} %get-tuple-element.16.refs_3_.refs_7_), channel_id=1, source_target_pairs={{0,12},{1,13},{2,14},{3,15},{4,8},{5,9},{6,10},{7,11},{8,4},{9,5},... | collective-permute-start | bytes 387080 | tf_op jit(solution)/shard_map/ppermute | solution.py:376
  9.7 20.3 %collective-permute-start.1 = (bf16[56,1152]{1,0:T(8,128)(2,1)S(1)}, bf16[56,1152]{1,0:T(8,128)(2,1)S(1)}, u32[]{:S(2)}, u32[]{:S(2)}) collective-permute-start(bf16[56,1152]{1,0:T(8,128)(2,1)S(1)} %get-tuple-element.16.refs_3_.refs_7_), channel_id=1, source_target_pairs={{0,8},{1,9},{2,10},{3,11},{4,12},{5,13},{6,14},{7,15},{8,0},{9,1},... | collective-permute-start | bytes 387080 | tf_op jit(solution)/shard_map/ppermute | solution.py:376
  9.7 20.3 %collective-permute-start = (bf16[56,1152]{1,0:T(8,128)(2,1)S(1)}, bf16[56,1152]{1,0:T(8,128)(2,1)S(1)}, u32[]{:S(2)}, u32[]{:S(2)}) collective-permute-start(bf16[56,1152]{1,0:T(8,128)(2,1)S(1)} %get-tuple-element.16.refs_3_.refs_7_), channel_id=1, source_target_pairs={{0,4},{1,5},{2,6},{3,7},{4,0},{5,1},{6,2},{7,3},{8,12},{9,13},{10,... | collective-permute-start | bytes 387080 | tf_op jit(solution)/shard_map/ppermute | solution.py:376
  10.5 8.4 %collective-permute-start.6 = (bf16[8,1152]{1,0:T(8,128)(2,1)S(1)}, bf16[8,1152]{1,0:T(8,128)(2,1)S(1)}, u32[]{:S(2)}, u32[]{:S(2)}) collective-permute-start(bf16[8,1152]{1,0:T(8,128)(2,1)S(1)} %get-tuple-element.15.refs_0_), channel_id=1, source_target_pairs={{0,14},{1,15},{2,12},{3,13},{4,10},{5,11},{6,8},{7,9},{8,6},{9,7},... | collective-permute-start | bytes 55304 | tf_op jit(solution)/shard_map/ppermute | solution.py:376
  18.9 6.4 %collective-permute-start.5 = (bf16[8,1152]{1,0:T(8,128)(2,1)S(1)}, bf16[8,1152]{1,0:T(8,128)(2,1)S(1)}, u32[]{:S(2)}, u32[]{:S(2)}) collective-permute-start(bf16[8,1152]{1,0:T(8,128)(2,1)S(1)} %get-tuple-element.15.refs_0_), channel_id=1, source_target_pairs={{0,10},{1,11},{2,8},{3,9},{4,14},{5,15},{6,12},{7,13},{8,2},{9,3},... | collective-permute-start | bytes 55304 | tf_op jit(solution)/shard_map/ppermute | solution.py:376
  25.3 4.7 %collective-permute-start.4 = (bf16[8,1152]{1,0:T(8,128)(2,1)S(1)}, bf16[8,1152]{1,0:T(8,128)(2,1)S(1)}, u32[]{:S(2)}, u32[]{:S(2)}) collective-permute-start(bf16[8,1152]{1,0:T(8,128)(2,1)S(1)} %get-tuple-element.15.refs_0_), channel_id=1, source_target_pairs={{0,6},{1,7},{2,4},{3,5},{4,2},{5,3},{6,0},{7,1},{8,14},{9,15},{10,... | collective-permute-start | bytes 55304 | tf_op jit(solution)/shard_map/ppermute | solution.py:376
  30.0 4.1 %collective-permute-start.8 = (bf16[56,1152]{1,0:T(8,128)(2,1)S(1)}, bf16[56,1152]{1,0:T(8,128)(2,1)S(1)}, u32[]{:S(2)}, u32[]{:S(2)}) collective-permute-start(bf16[56,1152]{1,0:T(8,128)(2,1)S(1)} %get-tuple-element.16.refs_3_.refs_7_), channel_id=1, source_target_pairs={{0,1},{1,0},{2,3},{3,2},{4,5},{5,4},{6,7},{7,6},{8,9},{9,8},{10,11... | collective-permute-start | bytes 387080 | tf_op jit(solution)/shard_map/ppermute | solution.py:376
  30.1 4.0 %collective-permute-start.7 = (f32[8,1152]{1,0:T(8,128)S(1)}, f32[8,1152]{1,0:T(8,128)S(1)}, u32[]{:S(2)}, u32[]{:S(2)}) collective-permute-start(f32[8,1152]{1,0:T(8,128)S(1)} %add.1.refs_1_.sums_a), channel_id=1, source_target_pairs={{0,1},{1,0},{2,3},{3,2},{4,5},{5,4},{6,7},{7,6},{8,9},{9,8},{10,11... | collective-permute-start | bytes 110600 | tf_op jit(solution)/shard_map/ppermute | solution.py:376
  30.7 3.5 %collective-permute-start.9 = (bf16[56,1152]{1,0:T(8,128)(2,1)S(1)}, bf16[56,1152]{1,0:T(8,128)(2,1)S(1)}, u32[]{:S(2)}, u32[]{:S(2)}) collective-permute-start(bf16[56,1152]{1,0:T(8,128)(2,1)S(1)} %collective-permute-done.3.refs_4_.refs_8_), channel_id=1, source_target_pairs={{0,1},{1,0},{2,3},{3,2},{4,5},{5,4},{6,7},{7,6},{8,9},{9,8},{10,11... | collective-permute-start | bytes 387080 | tf_op jit(solution)/shard_map/ppermute | solution.py:376
  34.1 12.1 %copy-start = (bf16[1152,1152]{1,0:T(8,128)(2,1)S(1)}, bf16[1152,1152]{1,0:T(8,128)(2,1)}, u32[]{:S(2)}) copy-start(bf16[1152,1152]{1,0:T(8,128)(2,1)} %weight.1) | copy-start | bytes 7962628
  38.4 1.6 %collective-permute-start.10 = (bf16[96,1280]{1,0:T(8,128)(2,1)S(1)}, bf16[96,1280]{1,0:T(8,128)(2,1)S(1)}, u32[]{:S(2)}, u32[]{:S(2)}) collective-permute-start(bf16[96,1280]{1,0:T(8,128)(2,1)S(1)} %get-tuple-element.19), channel_id=1, source_target_pairs={{0,1},{1,0},{2,3},{3,2},{4,5},{5,4},{6,7},{7,6},{8,9},{9,8},{10,11... | collective-permute-start | bytes 737288 | tf_op jit(solution)/shard_map/ppermute | solution.py:376
  40.5 5.7 %collective-permute-start.11 = (bf16[48,1280]{1,0:T(8,128)(2,1)S(1)}, bf16[48,1280]{1,0:T(8,128)(2,1)S(1)}, u32[]{:S(2)}, u32[]{:S(2)}) collective-permute-start(bf16[48,1280]{1,0:T(8,128)(2,1)S(1)} %get-tuple-element.21), channel_id=1, source_target_pairs={{0,2},{1,3},{2,0},{3,1},{4,6},{5,7},{6,4},{7,5},{8,10},{9,11},{10,... | collective-permute-start | bytes 368648 | tf_op jit(solution)/shard_map/ppermute | solution.py:376
where the time goes:
time: 48 us; the launch traced here: 47.8 us
  starting transfers between devices  20.5 us (43%)
  waiting for transfers between devices  14.4 us (30%)
  Pallas kernels  12.2 us (25%)
  between operations  0.75 us (2%)
    ppermute x12, starting transfers between devices, swap(): return lax.ppermute(value, 'patch', pairs)  20.5 us
    ppermute x12, waiting for transfers between devices, swap(): return lax.ppermute(value, 'patch', pairs)  14.4 us
    pallas_call x1, Pallas kernels, per_device(): pl.pallas_call(functools.partial(attend_kernel, rows, len(key_parts)), ou...  4.26 us
    pallas_call x1, Pallas kernels, per_device(): weight = load(row_valid, stay_far(qkv_weight))  3.35 us
    pallas_call x1, Pallas kernels, per_device(): pl.pallas_call(functools.partial(front_kernel, part_index, len(key_masks)...  2.43 us
    pallas_call x1, Pallas kernels, per_device(): pl.pallas_call(finish_kernel, out_shape=shape((rows, width), jnp.bfloat16...  1.62 us
  transfers between devices with their start and end apart: 12, of which 5 were waited for; matrix products, arithmetic and copies ran while one was open for 0% of the time, Pallas kernels for 7%

commit v1 on v0

v1 whole, which is shorter than its diff:
```python
import functools
import math

import jax
import jax.numpy as jnp
import numpy as np
from jax import lax
from jax.experimental import pallas as pl
from jax.experimental.pallas import tpu as pltpu
from jax.sharding import PartitionSpec as P


HEADS = 16
LANES = 128
SUM_ROWS = 8
CORE_MASK = 1
MERGE_MASK = 2
DIRECT_LIMIT = 16
ATTEND_GRANT = 24
neg_large = -1e30


def grant(mebibytes):
    return pltpu.CompilerParams(vmem_limit_bytes=mebibytes << 20)


def vmem():
    return pl.BlockSpec(memory_space=pltpu.VMEM)


def lane_table(model_width, freq_size):
    quarter = model_width // 4
    half = freq_size // 2
    lane = np.arange(model_width)
    table = np.zeros((SUM_ROWS, model_width), np.float32)
    table[0] = np.power(10000.0, -(lane % quarter) / quarter)
    table[1] = (lane // quarter) % 2
    table[2] = lane // (2 * quarter)
    feature = np.arange(freq_size)
    table[3, :freq_size] = np.exp(-math.log(10000.0) * (feature % half) / half)
    table[4, :freq_size] = feature < half
    return table


def sine(angle, shifted):
    turns = jnp.floor(angle * (0.5 / math.pi) + 0.5)
    rest = angle - turns * 6.28125
    rest = rest - turns * (2.0 * math.pi - 6.28125)
    rest = rest + shifted * (0.5 * math.pi)
    rest = jnp.where(rest > 0.5 * math.pi, math.pi - rest, rest)
    rest = jnp.where(rest < -0.5 * math.pi, -math.pi - rest, rest)
    square = rest * rest
    series = 1.0 / math.factorial(13)
    for power in (11, 9, 7, 5, 3, 1):
        sign = -1.0 if power % 4 == 3 else 1.0
        series = series * square + sign / math.factorial(power)
    return rest * series


def silu(value):
    return value / (1.0 + jnp.exp(-value))


def high_low(value):
    high = value.astype(jnp.bfloat16)
    return high, (value - high.astype(jnp.float32)).astype(jnp.bfloat16)


def front_kernel(
    part_index,
    parts,
    timestep,
    counts_far,
    tokens_far,
    positions_far,
    table_far,
    time_in_far,
    time_out_far,
    ada_weight_far,
    message,
    sums,
    x_in_ref,
    bias,
    row_valid,
    counts,
    tokens,
    positions,
    table,
    time_in,
    time_out,
    ada_weight,
    arrived,
):
    order = (
        (table_far, table),
        (time_in_far, time_in),
        (time_out_far, time_out),
        (ada_weight_far, ada_weight),
        (positions_far, positions),
        (tokens_far, tokens),
        (counts_far, counts),
    )
    copies = [
        pltpu.make_async_copy(far, near, arrived.at[index])
        for index, (far, near) in enumerate(order)
    ]
    for copy in copies:
        copy.start()
    rows, width = tokens.shape
    freq_size = time_in.shape[0]
    copies[0].wait()
    angle = timestep[0].astype(jnp.float32) * jnp.broadcast_to(
        table[3:4, :freq_size], (SUM_ROWS, freq_size)
    )
    shifted = jnp.broadcast_to(table[4:5, :freq_size], (SUM_ROWS, freq_size))
    features = sine(angle, shifted).astype(jnp.bfloat16)
    copies[1].wait()
    hidden = silu(jnp.dot(features, time_in[...], preferred_element_type=jnp.float32))
    copies[2].wait()
    cond = lax.dot_general(
        hidden.astype(jnp.bfloat16),
        time_out[...],
        (((1,), (1,)), ((), ())),
        preferred_element_type=jnp.float32,
    )
    copies[3].wait()
    partial = jnp.dot(
        silu(cond).astype(jnp.bfloat16), ada_weight[...], preferred_element_type=jnp.float32
    )
    sums[...] = pack_sums([partial[:, piece * width : (piece + 1) * width] for piece in range(3)])

    copies[4].wait()
    place = positions[...].astype(jnp.float32)
    same = lax.broadcasted_iota(jnp.int32, (rows, rows), 0) == lax.broadcasted_iota(
        jnp.int32, (rows, rows), 1
    )
    column = [
        jnp.sum(jnp.where(same, place[axis : axis + 1, :], 0.0), axis=1, keepdims=True)
        for axis in range(2)
    ]
    where_to = jnp.where(table[2:3, :] > 0.5, column[1], column[0])
    embed = sine(where_to * table[0:1, :], table[1:2, :])
    copies[5].wait()
    x_in = tokens[...].astype(jnp.float32) + embed
    x_in_ref[...] = x_in
    centered = x_in - jnp.mean(x_in, axis=1, keepdims=True)
    variance = jnp.mean(centered * centered, axis=1, keepdims=True)
    message[...] = (centered * lax.rsqrt(variance + 1e-06)).astype(jnp.bfloat16)

    copies[6].wait()
    my_index = lax.axis_index("patch")
    key_id = lax.broadcasted_iota(jnp.int32, bias.shape, 1)
    valid = key_id < 0
    for block in range(parts):
        first = block * rows
        used = counts[part_index(my_index, block)]
        valid = jnp.logical_or(valid, jnp.logical_and(key_id >= first, key_id < first + used))
    bias[...] = jnp.where(valid, 0.0, neg_large)
    own_row = lax.broadcasted_iota(jnp.int32, row_valid.shape, 0)
    row_valid[...] = (own_row < counts[my_index]).astype(jnp.float32)


def pack_sums(pieces):
    row_id = lax.broadcasted_iota(jnp.int32, pieces[0].shape, 0)
    packed = jnp.zeros(pieces[0].shape, jnp.float32)
    for piece, value in enumerate(pieces):
        high, low = high_low(value)
        packed = jnp.where(row_id == 2 * piece, high.astype(jnp.float32), packed)
        packed = jnp.where(row_id == 2 * piece + 1, low.astype(jnp.float32), packed)
    return packed.astype(jnp.bfloat16)


def sum_piece(value, piece):
    return value[2 * piece : 2 * piece + 1, :] + value[2 * piece + 1 : 2 * piece + 2, :]


def add_kernel(*refs):
    out = refs[-1]
    total = sum(ref[...].astype(jnp.float32) for ref in refs[:-1])
    out[...] = pack_sums(
        [jnp.broadcast_to(sum_piece(total, piece), out.shape) for piece in range(3)]
    )


def attend_rows(query_ref, start, rows, key_bias, keys, values, out):
    width = keys.shape[1]
    head_size = width // HEADS
    base_two = math.log2(math.e) / math.sqrt(head_size)
    lse_lane = lax.broadcasted_iota(jnp.int32, (rows, LANES), 1)
    lse_all = jnp.zeros((rows, LANES), jnp.float32)
    held = None
    tiles = []
    for group in head_groups(width):
        low, high = group[0] * head_size, (group[-1] + 1) * head_size
        first, last = low // LANES * LANES, -(-high // LANES) * LANES
        lane = lax.broadcasted_iota(jnp.int32, (1, last - first), 1) + first
        window = query_ref[start : start + rows, first:last]
        stacked = jnp.concatenate(
            [
                jnp.where(
                    jnp.logical_and(lane >= head * head_size, lane < (head + 1) * head_size),
                    window,
                    jnp.zeros((), jnp.bfloat16),
                )
                for head in group
            ],
            axis=0,
        )
        scores = lax.dot_general(
            stacked,
            keys[:, first:last],
            (((1,), (1,)), ((), ())),
            preferred_element_type=jnp.float32,
        )
        scores = scores + key_bias
        top = jnp.max(scores, axis=1, keepdims=True)
        weights = jnp.exp2((scores - top) * base_two)
        total = jnp.sum(weights, axis=1, keepdims=True)
        result = jnp.dot(
            weights.astype(jnp.bfloat16), values[:, first:last], preferred_element_type=jnp.float32
        )
        result = result * (1.0 / total)
        lse = top * base_two + jnp.log2(total)
        joined = result[:rows, :]
        for place, head in enumerate(group):
            mine = slice(place * rows, (place + 1) * rows)
            lse_all = jnp.where(lse_lane == head, lse[mine, :], lse_all)
            if place:
                joined = jnp.where(lane >= head * head_size, result[mine, :], joined)
        for begin in range(first, last, LANES):
            tile = joined[:, begin - first : begin - first + LANES]
            if begin < low:
                tile = jnp.where(lane[:, begin - first : begin - first + LANES] >= low, tile, held)
            if begin + LANES <= high:
                tiles.append(tile.astype(jnp.bfloat16))
            else:
                held = tile
    tiles.append(pack_lse(lse_all))
    for index, tile in enumerate(tiles):
        out[:, index * LANES : (index + 1) * LANES] = tile


def head_groups(width):
    head_size = width // HEADS
    groups = []
    head = 0
    while head < HEADS:
        first = head * head_size // LANES * LANES
        stop = head + 1
        while stop < HEADS and (stop + 1) * head_size <= first + 2 * LANES:
            stop += 1
        groups.append(tuple(range(head, stop)))
        head = stop
    return groups


def attend_kernel(block_rows, key_count, *refs):
    bias, sums_a, sums_b = refs[:3]
    key_refs = refs[3 : 3 + key_count]
    own, across, weight = refs[3 + key_count : 6 + key_count]
    own_query, keys, values, across_out = refs[6 + key_count : 10 + key_count]
    mod_keys, mod_queries, across_query = refs[10 + key_count :]
    width = weight.shape[0]
    sums = sums_a[...].astype(jnp.float32) + sums_b[...].astype(jnp.float32)
    shift = sum_piece(sums, 0)
    scale = 1.0 + sum_piece(sums, 1)

    def modulate(value):
        return (value.astype(jnp.float32) * scale + shift).astype(jnp.bfloat16)

    place = 0
    for ref in key_refs:
        for start in range(0, ref.shape[0], block_rows):
            mod_keys[place : place + block_rows, :] = modulate(ref[start : start + block_rows, :])
            place += block_rows
    mod_queries[:block_rows, :] = modulate(own[...])
    mod_queries[block_rows:, :] = modulate(across[...])
    piece = 3 * LANES
    for start in range(0, width, piece):
        stop = min(start + piece, width)
        both = jnp.dot(
            mod_queries[...], weight[:, start:stop], preferred_element_type=jnp.float32
        ).astype(jnp.bfloat16)
        own_query[:, start:stop] = both[:block_rows, :]
        across_query[:, start:stop] = both[block_rows:, :]
        keys[:, start:stop] = jnp.dot(
            mod_keys[...], weight[:, width + start : width + stop], preferred_element_type=jnp.float32
        ).astype(jnp.bfloat16)
        values[:, start:stop] = jnp.dot(
            mod_keys[...],
            weight[:, 2 * width + start : 2 * width + stop],
            preferred_element_type=jnp.float32,
        ).astype(jnp.bfloat16)
    attend_rows(across_query, 0, block_rows, bias[0:1, :], keys, values, across_out)


def own_kernel(bias, query, keys, values, out):
    attend_rows(query, 0, query.shape[0], bias[0:1, :], keys, values, out)


def pack_lse(lse):
    high = lse.astype(jnp.bfloat16).astype(jnp.float32)
    middle = (lse - high).astype(jnp.bfloat16).astype(jnp.float32)
    low = lse - high - middle
    return (high + pltpu.roll(middle, HEADS, 1) + pltpu.roll(low, 2 * HEADS, 1)).astype(
        jnp.bfloat16
    )


def unpack_lse(packed):
    source = lax.broadcasted_iota(jnp.int32, (LANES, LANES), 0)
    target = lax.broadcasted_iota(jnp.int32, (LANES, LANES), 1)
    chosen = source == target
    for piece in range(1, 3):
        chosen = jnp.logical_or(chosen, source == target + piece * HEADS)
    chosen = jnp.logical_and(chosen, target < HEADS).astype(jnp.bfloat16)
    return jnp.dot(packed, chosen, preferred_element_type=jnp.float32)


def spread(value, width):
    head_size = width // HEADS
    head_id = lax.broadcasted_iota(jnp.int32, (LANES, width), 0)
    lane_id = lax.broadcasted_iota(jnp.int32, (LANES, width), 1)
    low = head_id * head_size
    expand = jnp.logical_and(lane_id >= low, lane_id < low + head_size).astype(jnp.bfloat16)
    high, rest = high_low(value)
    return jnp.dot(high, expand, preferred_element_type=jnp.float32) + jnp.dot(
        rest, expand, preferred_element_type=jnp.float32
    )


def merge(packed_a, packed_b):
    width = packed_a.shape[1] - LANES
    lse_a, lse_b = unpack_lse(packed_a[:, width:]), unpack_lse(packed_b[:, width:])
    top = jnp.maximum(lse_a, lse_b)
    part_a = jnp.exp2(lse_a - top)
    part_b = jnp.exp2(lse_b - top)
    total = part_a + part_b
    share = spread(part_b / total, width)
    first = packed_a[:, :width].astype(jnp.float32)
    value = first + share * (packed_b[:, :width].astype(jnp.float32) - first)
    return value


def finish_kernel(packed_a, packed_b, x_in, row_valid, sums_a, sums_b, weight, out):
    value = merge(packed_a[...], packed_b[...])
    gate = sum_piece(sums_a[...].astype(jnp.float32) + sums_b[...].astype(jnp.float32), 2)
    projected = jnp.dot(
        value.astype(jnp.bfloat16), weight[...], preferred_element_type=jnp.float32
    )
    out[...] = (x_in[...] + gate * projected * row_valid[:, 0:1]).astype(jnp.bfloat16)


def far():
    return pl.BlockSpec(memory_space=pltpu.HBM)


def stay_far(array):
    return pltpu.with_memory_space_constraint(array, pltpu.HBM)


def per_device(
    tokens, positions, counts, timestep, time_in, time_out, ada_weight, qkv_weight, out_weight
):
    devices = lax.axis_size("patch")
    rows, width = tokens.shape
    shape = jax.ShapeDtypeStruct
    table = jnp.asarray(lane_table(width, time_in.shape[0]))
    far_masks = [mask for mask in range(devices) if not mask & (CORE_MASK | MERGE_MASK)]
    key_masks = far_masks + [mask | CORE_MASK for mask in far_masks]
    direct = devices <= DIRECT_LIMIT

    def swap(value, mask):
        pairs = [(index, index ^ mask) for index in range(devices)]
        return lax.ppermute(value, "patch", pairs)

    def part_index(my_index, block):
        if direct:
            return jnp.bitwise_xor(my_index, key_masks[block])
        return jnp.bitwise_and(my_index, MERGE_MASK) + sorted(key_masks)[block]

    inputs = (timestep, counts, tokens, positions, table, time_in, time_out.T, ada_weight)
    message, sums, x_in, bias, row_valid = pl.pallas_call(
        functools.partial(front_kernel, part_index, len(key_masks)),
        out_shape=(
            shape((rows, width), jnp.bfloat16),
            shape((SUM_ROWS, width), jnp.bfloat16),
            shape((rows, width), jnp.float32),
            shape((SUM_ROWS, rows * len(key_masks)), jnp.float32),
            shape((rows, LANES), jnp.float32),
        ),
        in_specs=[pl.BlockSpec(memory_space=pltpu.SMEM)] + [far()] * (len(inputs) - 1),
        out_specs=(vmem(),) * 5,
        scratch_shapes=[
            (pltpu.SMEM if array.ndim == 1 else pltpu.VMEM)(array.shape, array.dtype)
            for array in inputs[1:]
        ]
        + [pltpu.SemaphoreType.DMA((len(inputs) - 1,))],
        compiler_params=grant(8),
        name="front",
    )(inputs[0], *[stay_far(array) for array in inputs[1:]])

    def add(*addends):
        return pl.pallas_call(
            add_kernel,
            out_shape=shape((SUM_ROWS, width), jnp.bfloat16),
            in_specs=[vmem()] * len(addends),
            out_specs=vmem(),
            compiler_params=grant(4),
            cost_estimate=pl.CostEstimate(
                flops=1 << 34, bytes_accessed=4 * qkv_weight.size, transcendentals=0
            ),
            name="add",
        )(*addends)

    across = swap(message, MERGE_MASK)
    if direct:
        near = [message] + [swap(message, mask) for mask in far_masks[1:]]
        key_parts = near + [swap(part, CORE_MASK) for part in near]
        running = add(sums, swap(sums, CORE_MASK))
        running = add(running, *[swap(running, mask) for mask in far_masks[1:]])
        half_sums = running
        other_sums = swap(running, MERGE_MASK)
    else:
        groups = [[mask | rest for mask in sorted(key_masks)] for rest in (0, MERGE_MASK)]
        key_parts = [lax.all_gather(message, "patch", axis_index_groups=groups, tiled=True)]
        running = sums
        step = 1
        while 2 * step < devices:
            running = add(running, swap(running, step))
            step *= 2
        half_sums = running
        other_sums = swap(running, step)

    total_keys = rows * len(key_masks)
    own_query, keys, values, send = pl.pallas_call(
        functools.partial(attend_kernel, rows, len(key_parts)),
        out_shape=(
            shape((rows, width), jnp.bfloat16),
            shape((total_keys, width), jnp.bfloat16),
            shape((total_keys, width), jnp.bfloat16),
            shape((rows, width + LANES), jnp.bfloat16),
        ),
        in_specs=[vmem()] * (6 + len(key_parts)),
        out_specs=(vmem(),) * 4,
        scratch_shapes=[
            pltpu.VMEM((total_keys, width), jnp.bfloat16),
            pltpu.VMEM((2 * rows, width), jnp.bfloat16),
            pltpu.VMEM((rows, width), jnp.bfloat16),
        ],
        compiler_params=grant(ATTEND_GRANT if direct else 56),
        name="attend",
    )(bias, half_sums, other_sums, *key_parts, message, across, qkv_weight)
    own = pl.pallas_call(
        own_kernel,
        out_shape=shape((rows, width + LANES), jnp.bfloat16),
        in_specs=[vmem()] * 4,
        out_specs=vmem(),
        compiler_params=grant(8 if direct else 40),
        cost_estimate=pl.CostEstimate(
            flops=1 << 34, bytes_accessed=4 * keys.size, transcendentals=0
        ),
        name="own",
    )(bias, own_query, keys, values)
    return pl.pallas_call(
        finish_kernel,
        out_shape=shape((rows, width), jnp.bfloat16),
        in_specs=[vmem()] * 7,
        out_specs=vmem(),
        compiler_params=grant(8),
        name="finish",
    )(own, swap(send, MERGE_MASK), x_in, row_valid, half_sums, other_sums, out_weight)


def solution(mesh):
    placed = (
        P(("req", "patch"), None),
        P(None, ("req", "patch")),
        P("req"),
        P("req"),
        P(),
        P(None, "patch"),
        P("patch", None),
        P(),
        P(),
    )

    return jax.shard_map(
        per_device, mesh=mesh, in_specs=placed, out_specs=P(("req", "patch"), None), check_vma=False
    )
```

time: 48 us -> 37.4 us (0.78)
  starting transfers between devices: 20.5 us -> 15.3 us
  waiting for transfers between devices: 14.4 us -> 9.25 us
    ppermute x12 -> x14, starting transfers between devices: 20.5 us -> 15.3 us  [swap(): return lax.ppermute(value, 'patch', pairs)]
    ppermute x12 -> x14, waiting for transfers between devices: 14.4 us -> 9.25 us  [swap(): return lax.ppermute(value, 'patch', pairs)]
    pallas_call x3, Pallas kernels: 3.88 us -> 2.48 us  [the longest x1 2.4 us: per_device(): pl.pallas_call(own_kernel, out_shape=shape((rows, width + LANES), jnp.bfl...]
    pallas_call x1, Pallas kernels: 4.26 us -> 5.53 us  [per_device(): pl.pallas_call(functools.partial(attend_kernel, rows, len(key_parts)), ou...]
  transfers between devices with their start and end apart: 12 -> 14, of which waited for: 5 -> 6; matrix products, arithmetic and copies ran while one was open for 0% -> 0% of each run, Pallas kernels for 7% -> 7%
where the time goes in v1:
time: 37.4 us; the launch traced here: 37.3 us
  starting transfers between devices  15.3 us (41%)
  Pallas kernels  12.1 us (32%)
  waiting for transfers between devices  9.25 us (25%)
  between operations  0.7 us (2%)
    ppermute x14, starting transfers between devices, swap(): return lax.ppermute(value, 'patch', pairs)  15.3 us
    ppermute x14, waiting for transfers between devices, swap(): return lax.ppermute(value, 'patch', pairs)  9.25 us
    pallas_call x1, Pallas kernels, per_device(): pl.pallas_call(functools.partial(attend_kernel, rows, len(key_parts)), ou...  5.53 us
    pallas_call x1, Pallas kernels, per_device(): pl.pallas_call(functools.partial(front_kernel, part_index, len(key_masks)...  2.44 us
    pallas_call x1, Pallas kernels, per_device(): pl.pallas_call(own_kernel, out_shape=shape((rows, width + LANES), jnp.bfl...  2.4 us
    pallas_call x1, Pallas kernels, per_device(): pl.pallas_call(finish_kernel, out_shape=shape((rows, width), jnp.bfloat16...  1.62 us
  transfers between devices with their start and end apart: 14, of which 6 were waited for; matrix products, arithmetic and copies ran while one was open for 0% of the time, Pallas kernels for 7%

profile of v1, /device:TPU:0, one launch (start us, length us, event | category | flops | bytes accessed | tf_op | source)
XLA Modules:
  0.0 37.3 jit_solution(11076486908414754108)
XLA Ops:
  0.7 2.4 %front.1 = (bf16[48,1152]{1,0:T(8,128)(2,1)S(1)}, bf16[8,1152]{1,0:T(8,128)(2,1)S(1)}, f32[48,1152]{1,0:T(8,128)S(1)}, f32[8,384]{1,0:T(8,128)S(1)}, f32[48,128]{1,0:T(8,128)S(1)}) custom-call(s32[1]{0:T(128)S(6)} %copy.11.timestep, s32[16]{0:T(128)} %counts_far.1, bf16[48,1152]{1,0:T(8,128)(2,1)} %tokens_far.1, s32[2,48]{1,0:T(2,128)} %positions_far.1, ...), custom_call_target="tpu_custom_call" | custom-call | tf_op jit(solution)/shard_map/front/pallas_call | solution.py:383
  3.1 0.6 %collective-permute-start = (bf16[8,1152]{1,0:T(8,128)(2,1)S(1)}, bf16[8,1152]{1,0:T(8,128)(2,1)S(1)}, u32[]{:S(2)}, u32[]{:S(2)}) collective-permute-start(bf16[8,1152]{1,0:T(8,128)(2,1)S(1)} %get-tuple-element.15.refs_0_), channel_id=1, source_target_pairs={{0,1},{1,0},{2,3},{3,2},{4,5},{5,4},{6,7},{7,6},{8,9},{9,8},{10,11... | collective-permute-start | bytes 55304 | tf_op jit(solution)/shard_map/ppermute | solution.py:375
  3.7 0.8 %collective-permute-done.refs_1_ = bf16[8,1152]{1,0:T(8,128)(2,1)S(1)} collective-permute-done((bf16[8,1152]{1,0:T(8,128)(2,1)S(1)}, bf16[8,1152]{1,0:T(8,128)(2,1)S(1)}, u32[]{:S(2)}, u32[]{:S(2)}) %collective-permute-start) | collective-permute-done | bytes 18464 | tf_op jit(solution)/shard_map/ppermute | solution.py:375
  4.5 5.0 %collective-permute-start.3 = (bf16[8,1152]{1,0:T(8,128)(2,1)S(1)}, bf16[8,1152]{1,0:T(8,128)(2,1)S(1)}, u32[]{:S(2)}, u32[]{:S(2)}) collective-permute-start(bf16[8,1152]{1,0:T(8,128)(2,1)S(1)} %add.2.refs_0_), channel_id=1, source_target_pairs={{0,12},{1,13},{2,14},{3,15},{4,8},{5,9},{6,10},{7,11},{8,4},{9,5},... | collective-permute-start | bytes 55304 | tf_op jit(solution)/shard_map/ppermute | solution.py:375
  9.5 0.0 collective-permute-start.2
  9.5 0.6 %collective-permute-start.1 = (bf16[8,1152]{1,0:T(8,128)(2,1)S(1)}, bf16[8,1152]{1,0:T(8,128)(2,1)S(1)}, u32[]{:S(2)}, u32[]{:S(2)}) collective-permute-start(bf16[8,1152]{1,0:T(8,128)(2,1)S(1)} %add.2.refs_0_), channel_id=1, source_target_pairs={{0,4},{1,5},{2,6},{3,7},{4,0},{5,1},{6,2},{7,3},{8,12},{9,13},{10,... | collective-permute-start | bytes 55304 | tf_op jit(solution)/shard_map/ppermute | solution.py:375
  10.2 3.7 %collective-permute-start.7 = (bf16[48,1152]{1,0:T(8,128)(2,1)S(1)}, bf16[48,1152]{1,0:T(8,128)(2,1)S(1)}, u32[]{:S(2)}, u32[]{:S(2)}) collective-permute-start(bf16[48,1152]{1,0:T(8,128)(2,1)S(1)} %get-tuple-element.16.refs_3_.refs_11_), channel_id=1, source_target_pairs={{0,12},{1,13},{2,14},{3,15},{4,8},{5,9},{6,10},{7,11},{8,4},{9,5},... | collective-permute-start | bytes 331784 | tf_op jit(solution)/shard_map/ppermute | solution.py:375
  13.9 0.0 collective-permute-start.6
  13.9 0.0 collective-permute-done.3.refs_3_
  13.9 0.6 %collective-permute-start.5 = (bf16[48,1152]{1,0:T(8,128)(2,1)S(1)}, bf16[48,1152]{1,0:T(8,128)(2,1)S(1)}, u32[]{:S(2)}, u32[]{:S(2)}) collective-permute-start(bf16[48,1152]{1,0:T(8,128)(2,1)S(1)} %get-tuple-element.16.refs_3_.refs_11_), channel_id=1, source_target_pairs={{0,4},{1,5},{2,6},{3,7},{4,0},{5,1},{6,2},{7,3},{8,12},{9,13},{10,... | collective-permute-start | bytes 331784 | tf_op jit(solution)/shard_map/ppermute | solution.py:375
  14.6 0.0 collective-permute-done.2.refs_2_
  14.6 0.0 collective-permute-done.1.refs_1_
  14.6 1.7 %collective-permute-start.4 = (bf16[8,1152]{1,0:T(8,128)(2,1)S(1)}, bf16[8,1152]{1,0:T(8,128)(2,1)S(1)}, u32[]{:S(2)}, u32[]{:S(2)}) collective-permute-start(bf16[8,1152]{1,0:T(8,128)(2,1)S(1)} %add.3.refs_1_.sums_a), channel_id=1, source_target_pairs={{0,2},{1,3},{2,0},{3,1},{4,6},{5,7},{6,4},{7,5},{8,10},{9,11},{10,... | collective-permute-start | bytes 55304 | tf_op jit(solution)/shard_map/ppermute | solution.py:375
  16.3 0.4 %collective-permute-start.12 = (bf16[48,1152]{1,0:T(8,128)(2,1)S(1)}, bf16[48,1152]{1,0:T(8,128)(2,1)S(1)}, u32[]{:S(2)}, u32[]{:S(2)}) collective-permute-start(bf16[48,1152]{1,0:T(8,128)(2,1)S(1)} %get-tuple-element.16.refs_3_.refs_11_), channel_id=1, source_target_pairs={{0,2},{1,3},{2,0},{3,1},{4,6},{5,7},{6,4},{7,5},{8,10},{9,11},{10,... | collective-permute-start | bytes 331784 | tf_op jit(solution)/shard_map/ppermute | solution.py:375
  16.7 1.9 %collective-permute-done.4.refs_2_.sums_b = bf16[8,1152]{1,0:T(8,128)(2,1)S(1)} collective-permute-done((bf16[8,1152]{1,0:T(8,128)(2,1)S(1)}, bf16[8,1152]{1,0:T(8,128)(2,1)S(1)}, u32[]{:S(2)}, u32[]{:S(2)}) %collective-permute-start.4) | collective-permute-done | bytes 18464 | tf_op jit(solution)/shard_map/ppermute | solution.py:375
  18.6 0.0 collective-permute-start.8
  18.6 0.0 collective-permute-done.7.refs_6_
  18.7 0.5 %collective-permute-start.11 = (bf16[48,1152]{1,0:T(8,128)(2,1)S(1)}, bf16[48,1152]{1,0:T(8,128)(2,1)S(1)}, u32[]{:S(2)}, u32[]{:S(2)}) collective-permute-start(bf16[48,1152]{1,0:T(8,128)(2,1)S(1)} %collective-permute-done.7.refs_6_), channel_id=1, source_target_pairs={{0,1},{1,0},{2,3},{3,2},{4,5},{5,4},{6,7},{7,6},{8,9},{9,8},{10,11... | collective-permute-start | bytes 331784 | tf_op jit(solution)/shard_map/ppermute | solution.py:375
  19.2 3.8 %collective-permute-done.6.refs_5_ = bf16[48,1152]{1,0:T(8,128)(2,1)S(1)} collective-permute-done((bf16[48,1152]{1,0:T(8,128)(2,1)S(1)}, bf16[48,1152]{1,0:T(8,128)(2,1)S(1)}, u32[]{:S(2)}, u32[]{:S(2)}) %collective-permute-start.6) | collective-permute-done | bytes 110624 | tf_op jit(solution)/shard_map/ppermute | solution.py:375
  23.0 0.0 collective-permute-start.10
  23.0 0.0 collective-permute-done.5.refs_4_
  23.0 0.5 %collective-permute-start.9 = (bf16[48,1152]{1,0:T(8,128)(2,1)S(1)}, bf16[48,1152]{1,0:T(8,128)(2,1)S(1)}, u32[]{:S(2)}, u32[]{:S(2)}) collective-permute-start(bf16[48,1152]{1,0:T(8,128)(2,1)S(1)} %collective-permute-done.5.refs_4_), channel_id=1, source_target_pairs={{0,1},{1,0},{2,3},{3,2},{4,5},{5,4},{6,7},{7,6},{8,9},{9,8},{10,11... | collective-permute-start | bytes 331784 | tf_op jit(solution)/shard_map/ppermute | solution.py:375
  23.5 0.0 collective-permute-done.12.refs_12_
  23.5 0.0 collective-permute-done.8.refs_7_
  23.5 0.0 collective-permute-done.11.refs_10_
  23.5 0.8 %collective-permute-done.10.refs_9_ = bf16[48,1152]{1,0:T(8,128)(2,1)S(1)} collective-permute-done((bf16[48,1152]{1,0:T(8,128)(2,1)S(1)}, bf16[48,1152]{1,0:T(8,128)(2,1)S(1)}, u32[]{:S(2)}, u32[]{:S(2)}) %collective-permute-start.10) | collective-permute-done | bytes 110624 | tf_op jit(solution)/shard_map/ppermute | solution.py:375
  24.3 0.2 collective-permute-done.9.refs_8_
  24.5 5.5 %attend.1 = (bf16[48,1152]{1,0:T(8,128)(2,1)S(1)}, bf16[384,1152]{1,0:T(8,128)(2,1)S(1)}, bf16[384,1152]{1,0:T(8,128)(2,1)S(1)}, bf16[48,1280]{1,0:T(8,128)(2,1)S(1)}) custom-call(f32[8,384]{1,0:T(8,128)S(1)} %get-tuple-element.14.refs_0_.bias, bf16[8,1152]{1,0:T(8,128)(2,1)S(1)} %add.3.refs_1_.sums_a, ...), custom_call_target="tpu_custom_call" | custom-call | tf_op jit(solution)/shard_map/attend/pallas_call | solution.py:436
  30.0 1.6 %collective-permute-start.13 = (bf16[48,1280]{1,0:T(8,128)(2,1)S(1)}, bf16[48,1280]{1,0:T(8,128)(2,1)S(1)}, u32[]{:S(2)}, u32[]{:S(2)}) collective-permute-start(bf16[48,1280]{1,0:T(8,128)(2,1)S(1)} %get-tuple-element.20), channel_id=1, source_target_pairs={{0,2},{1,3},{2,0},{3,1},{4,6},{5,7},{6,4},{7,5},{8,10},{9,11},{10,... | collective-permute-start | bytes 368648 | tf_op jit(solution)/shard_map/ppermute | solution.py:375
  31.6 2.4 %own.1.packed_a = bf16[48,1280]{1,0:T(8,128)(2,1)S(1)} custom-call(f32[8,384]{1,0:T(8,128)S(1)} %get-tuple-element.14.refs_0_.bias, bf16[48,1152]{1,0:T(8,128)(2,1)S(1)} %get-tuple-element.17.query, bf16[384,1152]{1,0:T(8,128)(2,1)S(1)} %get-tuple-element.18.keys, bf16[384,1152]{1,0:T(8,128)(2,1)S(1)} %get-tuple-element.19.values), custom_call_target="tpu_custom_call" | custom-call | flops 17179869184 | bytes 1769472 | tf_op jit(solution)/shard_map/own/pallas_call | solution.py:454
  34.0 1.7 %collective-permute-done.13.packed_b = bf16[48,1280]{1,0:T(8,128)(2,1)S(1)} collective-permute-done((bf16[48,1280]{1,0:T(8,128)(2,1)S(1)}, bf16[48,1280]{1,0:T(8,128)(2,1)S(1)}, u32[]{:S(2)}, u32[]{:S(2)}) %collective-permute-start.13) | collective-permute-done | bytes 122912 | tf_op jit(solution)/shard_map/ppermute | solution.py:375
  35.7 1.6 %finish.1 = bf16[48,1152]{1,0:T(8,128)(2,1)} custom-call(bf16[48,1280]{1,0:T(8,128)(2,1)S(1)} %own.1.packed_a, bf16[48,1280]{1,0:T(8,128)(2,1)S(1)} %collective-permute-done.13.packed_b, f32[48,1152]{1,0:T(8,128)S(1)} %get-tuple-element.21.x_in, f32[48,128]{1,0:T(8,128)S(1)} %get-tuple-element.22.row_valid, bf16[8,1152]{1,0:T(8,128)(2,1)S(1)} %add.3.refs_1_.sums_a, ...), custom_call_target="tpu_custom_call" | custom-call | tf_op jit(solution)/shard_map/finish/pallas_call | solution.py:465
  (9 shorter events, 0.1 us)
Async XLA Ops:
  3.1 1.4 %collective-permute-start = (bf16[8,1152]{1,0:T(8,128)(2,1)S(1)}, bf16[8,1152]{1,0:T(8,128)(2,1)S(1)}, u32[]{:S(2)}, u32[]{:S(2)}) collective-permute-start(bf16[8,1152]{1,0:T(8,128)(2,1)S(1)} %get-tuple-element.15.refs_0_), channel_id=1, source_target_pairs={{0,1},{1,0},{2,3},{3,2},{4,5},{5,4},{6,7},{7,6},{8,9},{9,8},{10,11... | collective-permute-start | bytes 55304 | tf_op jit(solution)/shard_map/ppermute | solution.py:375
  4.5 9.4 %collective-permute-start.3 = (bf16[8,1152]{1,0:T(8,128)(2,1)S(1)}, bf16[8,1152]{1,0:T(8,128)(2,1)S(1)}, u32[]{:S(2)}, u32[]{:S(2)}) collective-permute-start(bf16[8,1152]{1,0:T(8,128)(2,1)S(1)} %add.2.refs_0_), channel_id=1, source_target_pairs={{0,12},{1,13},{2,14},{3,15},{4,8},{5,9},{6,10},{7,11},{8,4},{9,5},... | collective-permute-start | bytes 55304 | tf_op jit(solution)/shard_map/ppermute | solution.py:375
  9.5 5.0 %collective-permute-start.2 = (bf16[8,1152]{1,0:T(8,128)(2,1)S(1)}, bf16[8,1152]{1,0:T(8,128)(2,1)S(1)}, u32[]{:S(2)}, u32[]{:S(2)}) collective-permute-start(bf16[8,1152]{1,0:T(8,128)(2,1)S(1)} %add.2.refs_0_), channel_id=1, source_target_pairs={{0,8},{1,9},{2,10},{3,11},{4,12},{5,13},{6,14},{7,15},{8,0},{9,1},... | collective-permute-start | bytes 55304 | tf_op jit(solution)/shard_map/ppermute | solution.py:375
  9.5 5.0 %collective-permute-start.1 = (bf16[8,1152]{1,0:T(8,128)(2,1)S(1)}, bf16[8,1152]{1,0:T(8,128)(2,1)S(1)}, u32[]{:S(2)}, u32[]{:S(2)}) collective-permute-start(bf16[8,1152]{1,0:T(8,128)(2,1)S(1)} %add.2.refs_0_), channel_id=1, source_target_pairs={{0,4},{1,5},{2,6},{3,7},{4,0},{5,1},{6,2},{7,3},{8,12},{9,13},{10,... | collective-permute-start | bytes 55304 | tf_op jit(solution)/shard_map/ppermute | solution.py:375
  10.2 14.3 %slice-start = ((s8[7962624]{0:T(1024)(128)(4,1)}), s8[4194304]{0:T(1024)(128)(4,1)S(1)}, s32[]{:S(2)}) async-start(s8[7962624]{0:T(1024)(128)(4,1)} %bitcast.1), calls=%async_computation | async-start | bytes 8388608
  10.2 14.3 %slice-start.1 = ((s8[7962624]{0:T(1024)(128)(4,1)}), s8[3768320]{0:T(1024)(128)(4,1)S(1)}, s32[]{:S(2)}) async-start(s8[7962624]{0:T(1024)(128)(4,1)} %bitcast.1), calls=%async_computation.1 | async-start | bytes 7536640
  10.2 8.5 %collective-permute-start.7 = (bf16[48,1152]{1,0:T(8,128)(2,1)S(1)}, bf16[48,1152]{1,0:T(8,128)(2,1)S(1)}, u32[]{:S(2)}, u32[]{:S(2)}) collective-permute-start(bf16[48,1152]{1,0:T(8,128)(2,1)S(1)} %get-tuple-element.16.refs_3_.refs_11_), channel_id=1, source_target_pairs={{0,12},{1,13},{2,14},{3,15},{4,8},{5,9},{6,10},{7,11},{8,4},{9,5},... | collective-permute-start | bytes 331784 | tf_op jit(solution)/shard_map/ppermute | solution.py:375
  13.9 9.1 %collective-permute-start.6 = (bf16[48,1152]{1,0:T(8,128)(2,1)S(1)}, bf16[48,1152]{1,0:T(8,128)(2,1)S(1)}, u32[]{:S(2)}, u32[]{:S(2)}) collective-permute-start(bf16[48,1152]{1,0:T(8,128)(2,1)S(1)} %get-tuple-element.16.refs_3_.refs_11_), channel_id=1, source_target_pairs={{0,8},{1,9},{2,10},{3,11},{4,12},{5,13},{6,14},{7,15},{8,0},{9,1},... | collective-permute-start | bytes 331784 | tf_op jit(solution)/shard_map/ppermute | solution.py:375
  13.9 9.1 %collective-permute-start.5 = (bf16[48,1152]{1,0:T(8,128)(2,1)S(1)}, bf16[48,1152]{1,0:T(8,128)(2,1)S(1)}, u32[]{:S(2)}, u32[]{:S(2)}) collective-permute-start(bf16[48,1152]{1,0:T(8,128)(2,1)S(1)} %get-tuple-element.16.refs_3_.refs_11_), channel_id=1, source_target_pairs={{0,4},{1,5},{2,6},{3,7},{4,0},{5,1},{6,2},{7,3},{8,12},{9,13},{10,... | collective-permute-start | bytes 331784 | tf_op jit(solution)/shard_map/ppermute | solution.py:375
  14.6 4.0 %collective-permute-start.4 = (bf16[8,1152]{1,0:T(8,128)(2,1)S(1)}, bf16[8,1152]{1,0:T(8,128)(2,1)S(1)}, u32[]{:S(2)}, u32[]{:S(2)}) collective-permute-start(bf16[8,1152]{1,0:T(8,128)(2,1)S(1)} %add.3.refs_1_.sums_a), channel_id=1, source_target_pairs={{0,2},{1,3},{2,0},{3,1},{4,6},{5,7},{6,4},{7,5},{8,10},{9,11},{10,... | collective-permute-start | bytes 55304 | tf_op jit(solution)/shard_map/ppermute | solution.py:375
  16.3 7.2 %collective-permute-start.12 = (bf16[48,1152]{1,0:T(8,128)(2,1)S(1)}, bf16[48,1152]{1,0:T(8,128)(2,1)S(1)}, u32[]{:S(2)}, u32[]{:S(2)}) collective-permute-start(bf16[48,1152]{1,0:T(8,128)(2,1)S(1)} %get-tuple-element.16.refs_3_.refs_11_), channel_id=1, source_target_pairs={{0,2},{1,3},{2,0},{3,1},{4,6},{5,7},{6,4},{7,5},{8,10},{9,11},{10,... | collective-permute-start | bytes 331784 | tf_op jit(solution)/shard_map/ppermute | solution.py:375
  18.6 4.9 %collective-permute-start.8 = (bf16[48,1152]{1,0:T(8,128)(2,1)S(1)}, bf16[48,1152]{1,0:T(8,128)(2,1)S(1)}, u32[]{:S(2)}, u32[]{:S(2)}) collective-permute-start(bf16[48,1152]{1,0:T(8,128)(2,1)S(1)} %get-tuple-element.16.refs_3_.refs_11_), channel_id=1, source_target_pairs={{0,1},{1,0},{2,3},{3,2},{4,5},{5,4},{6,7},{7,6},{8,9},{9,8},{10,11... | collective-permute-start | bytes 331784 | tf_op jit(solution)/shard_map/ppermute | solution.py:375
  18.7 4.9 %collective-permute-start.11 = (bf16[48,1152]{1,0:T(8,128)(2,1)S(1)}, bf16[48,1152]{1,0:T(8,128)(2,1)S(1)}, u32[]{:S(2)}, u32[]{:S(2)}) collective-permute-start(bf16[48,1152]{1,0:T(8,128)(2,1)S(1)} %collective-permute-done.7.refs_6_), channel_id=1, source_target_pairs={{0,1},{1,0},{2,3},{3,2},{4,5},{5,4},{6,7},{7,6},{8,9},{9,8},{10,11... | collective-permute-start | bytes 331784 | tf_op jit(solution)/shard_map/ppermute | solution.py:375
  23.0 1.3 %collective-permute-start.10 = (bf16[48,1152]{1,0:T(8,128)(2,1)S(1)}, bf16[48,1152]{1,0:T(8,128)(2,1)S(1)}, u32[]{:S(2)}, u32[]{:S(2)}) collective-permute-start(bf16[48,1152]{1,0:T(8,128)(2,1)S(1)} %collective-permute-done.6.refs_5_), channel_id=1, source_target_pairs={{0,1},{1,0},{2,3},{3,2},{4,5},{5,4},{6,7},{7,6},{8,9},{9,8},{10,11... | collective-permute-start | bytes 331784 | tf_op jit(solution)/shard_map/ppermute | solution.py:375
  23.0 1.5 %collective-permute-start.9 = (bf16[48,1152]{1,0:T(8,128)(2,1)S(1)}, bf16[48,1152]{1,0:T(8,128)(2,1)S(1)}, u32[]{:S(2)}, u32[]{:S(2)}) collective-permute-start(bf16[48,1152]{1,0:T(8,128)(2,1)S(1)} %collective-permute-done.5.refs_4_), channel_id=1, source_target_pairs={{0,1},{1,0},{2,3},{3,2},{4,5},{5,4},{6,7},{7,6},{8,9},{9,8},{10,11... | collective-permute-start | bytes 331784 | tf_op jit(solution)/shard_map/ppermute | solution.py:375
  30.0 5.7 %collective-permute-start.13 = (bf16[48,1280]{1,0:T(8,128)(2,1)S(1)}, bf16[48,1280]{1,0:T(8,128)(2,1)S(1)}, u32[]{:S(2)}, u32[]{:S(2)}) collective-permute-start(bf16[48,1280]{1,0:T(8,128)(2,1)S(1)} %get-tuple-element.20), channel_id=1, source_target_pairs={{0,2},{1,3},{2,0},{3,1},{4,6},{5,7},{6,4},{7,5},{8,10},{9,11},{10,... | collective-permute-start | bytes 368648 | tf_op jit(solution)/shard_map/ppermute | solution.py:375
  31.6 4.1 %copy-start = (bf16[1152,1152]{1,0:T(8,128)(2,1)S(1)}, bf16[1152,1152]{1,0:T(8,128)(2,1)}, u32[]{:S(2)}) copy-start(bf16[1152,1152]{1,0:T(8,128)(2,1)} %weight.1) | copy-start | bytes 7962628

commit v2 on v1

--- a/solution.py
+++ b/solution.py
@@ -93,10 +93,10 @@
 ):
     order = (
         (table_far, table),
+        (positions_far, positions),
         (time_in_far, time_in),
         (time_out_far, time_out),
         (ada_weight_far, ada_weight),
-        (positions_far, positions),
         (tokens_far, tokens),
         (counts_far, counts),
     )
@@ -108,28 +108,8 @@
         copy.start()
     rows, width = tokens.shape
     freq_size = time_in.shape[0]
-    copies[0].wait()
-    angle = timestep[0].astype(jnp.float32) * jnp.broadcast_to(
-        table[3:4, :freq_size], (SUM_ROWS, freq_size)
-    )
-    shifted = jnp.broadcast_to(table[4:5, :freq_size], (SUM_ROWS, freq_size))
-    features = sine(angle, shifted).astype(jnp.bfloat16)
-    copies[1].wait()
-    hidden = silu(jnp.dot(features, time_in[...], preferred_element_type=jnp.float32))
-    copies[2].wait()
-    cond = lax.dot_general(
-        hidden.astype(jnp.bfloat16),
-        time_out[...],
-        (((1,), (1,)), ((), ())),
-        preferred_element_type=jnp.float32,
-    )
-    copies[3].wait()
-    partial = jnp.dot(
-        silu(cond).astype(jnp.bfloat16), ada_weight[...], preferred_element_type=jnp.float32
-    )
-    sums[...] = pack_sums([partial[:, piece * width : (piece + 1) * width] for piece in range(3)])
-
-    copies[4].wait()
+    for copy in copies[:2]:
+        copy.wait()
     place = positions[...].astype(jnp.float32)
     same = lax.broadcasted_iota(jnp.int32, (rows, rows), 0) == lax.broadcasted_iota(
         jnp.int32, (rows, rows), 1
@@ -140,14 +120,30 @@
     ]
     where_to = jnp.where(table[2:3, :] > 0.5, column[1], column[0])
     embed = sine(where_to * table[0:1, :], table[1:2, :])
-    copies[5].wait()
+    angle = timestep[0].astype(jnp.float32) * jnp.broadcast_to(
+        table[3:4, :freq_size], (SUM_ROWS, freq_size)
+    )
+    shifted = jnp.broadcast_to(table[4:5, :freq_size], (SUM_ROWS, freq_size))
+    features = sine(angle, shifted).astype(jnp.bfloat16)
+    for copy in copies[2:]:
+        copy.wait()
+    hidden = silu(jnp.dot(features, time_in[...], preferred_element_type=jnp.float32))
+    cond = lax.dot_general(
+        hidden.astype(jnp.bfloat16),
+        time_out[...],
+        (((1,), (1,)), ((), ())),
+        preferred_element_type=jnp.float32,
+    )
+    partial = jnp.dot(
+        silu(cond).astype(jnp.bfloat16), ada_weight[...], preferred_element_type=jnp.float32
+    )
     x_in = tokens[...].astype(jnp.float32) + embed
-    x_in_ref[...] = x_in
     centered = x_in - jnp.mean(x_in, axis=1, keepdims=True)
     variance = jnp.mean(centered * centered, axis=1, keepdims=True)
     message[...] = (centered * lax.rsqrt(variance + 1e-06)).astype(jnp.bfloat16)
-
-    copies[6].wait()
+    x_in_ref[...] = x_in
+    sums[...] = pack_sums([partial[:, piece * width : (piece + 1) * width] for piece in range(3)])
+
     my_index = lax.axis_index("patch")
     key_id = lax.broadcasted_iota(jnp.int32, bias.shape, 1)
     valid = key_id < 0
@@ -182,76 +178,77 @@
     )
 
 
-def attend_rows(query_ref, start, rows, key_bias, keys, values, out):
+def attend_rows(query_ref, rows, key_bias, keys, values, out):
     width = keys.shape[1]
     head_size = width // HEADS
     base_two = math.log2(math.e) / math.sqrt(head_size)
     lse_lane = lax.broadcasted_iota(jnp.int32, (rows, LANES), 1)
     lse_all = jnp.zeros((rows, LANES), jnp.float32)
-    held = None
-    tiles = []
-    for group in head_groups(width):
-        low, high = group[0] * head_size, (group[-1] + 1) * head_size
-        first, last = low // LANES * LANES, -(-high // LANES) * LANES
+    windows = [(first, min(first + 2 * LANES, width)) for first in range(0, width, 2 * LANES)]
+    inside = [
+        [
+            head
+            for head in range(HEADS)
+            if head * head_size < last and (head + 1) * head_size > first
+        ]
+        for first, last in windows
+    ]
+    scores, weights, inverse, tiles = {}, {}, {}, []
+
+    def lanes_of(head, first, last):
         lane = lax.broadcasted_iota(jnp.int32, (1, last - first), 1) + first
-        window = query_ref[start : start + rows, first:last]
+        return jnp.logical_and(lane >= head * head_size, lane < (head + 1) * head_size)
+
+    def score(index):
+        first, last = windows[index]
+        window = query_ref[:, first:last]
         stacked = jnp.concatenate(
             [
-                jnp.where(
-                    jnp.logical_and(lane >= head * head_size, lane < (head + 1) * head_size),
-                    window,
-                    jnp.zeros((), jnp.bfloat16),
-                )
-                for head in group
+                jnp.where(lanes_of(head, first, last), window, jnp.zeros((), jnp.bfloat16))
+                for head in inside[index]
             ],
             axis=0,
         )
-        scores = lax.dot_general(
+        result = lax.dot_general(
             stacked,
             keys[:, first:last],
             (((1,), (1,)), ((), ())),
             preferred_element_type=jnp.float32,
         )
-        scores = scores + key_bias
-        top = jnp.max(scores, axis=1, keepdims=True)
-        weights = jnp.exp2((scores - top) * base_two)
-        total = jnp.sum(weights, axis=1, keepdims=True)
+        for place, head in enumerate(inside[index]):
+            part = result[place * rows : (place + 1) * rows, :]
+            scores[head] = scores[head] + part if head in scores else part
+
+    score(0)
+    for index, (first, last) in enumerate(windows):
+        if index + 1 < len(windows):
+            score(index + 1)
+        for head in inside[index]:
+            if head in weights:
+                continue
+            value = scores.pop(head) + key_bias
+            top = jnp.max(value, axis=1, keepdims=True)
+            value = jnp.exp2((value - top) * base_two)
+            total = jnp.sum(value, axis=1, keepdims=True)
+            weights[head] = value.astype(jnp.bfloat16)
+            inverse[head] = 1.0 / total
+            lse_all = jnp.where(lse_lane == head, top * base_two + jnp.log2(total), lse_all)
         result = jnp.dot(
-            weights.astype(jnp.bfloat16), values[:, first:last], preferred_element_type=jnp.float32
+            jnp.concatenate([weights[head] for head in inside[index]], axis=0),
+            values[:, first:last],
+            preferred_element_type=jnp.float32,
         )
-        result = result * (1.0 / total)
-        lse = top * base_two + jnp.log2(total)
-        joined = result[:rows, :]
-        for place, head in enumerate(group):
-            mine = slice(place * rows, (place + 1) * rows)
-            lse_all = jnp.where(lse_lane == head, lse[mine, :], lse_all)
-            if place:
-                joined = jnp.where(lane >= head * head_size, result[mine, :], joined)
-        for begin in range(first, last, LANES):
-            tile = joined[:, begin - first : begin - first + LANES]
-            if begin < low:
-                tile = jnp.where(lane[:, begin - first : begin - first + LANES] >= low, tile, held)
-            if begin + LANES <= high:
-                tiles.append(tile.astype(jnp.bfloat16))
+        joined = None
+        for place, head in enumerate(inside[index]):
+            part = result[place * rows : (place + 1) * rows, :] * inverse[head]
+            if joined is None:
+                joined = part
             else:
-                held = tile
-    tiles.append(pack_lse(lse_all))
-    for index, tile in enumerate(tiles):
-        out[:, index * LANES : (index + 1) * LANES] = tile
-
-
-def head_groups(width):
-    head_size = width // HEADS
-    groups = []
-    head = 0
-    while head < HEADS:
-        first = head * head_size // LANES * LANES
-        stop = head + 1
-        while stop < HEADS and (stop + 1) * head_size <= first + 2 * LANES:
-            stop += 1
-        groups.append(tuple(range(head, stop)))
-        head = stop
-    return groups
+                joined = jnp.where(lanes_of(head, first, last), part, joined)
+        tiles.append((first, last, joined.astype(jnp.bfloat16)))
+    for first, last, tile in tiles:
+        out[:, first:last] = tile
+    out[:, width:] = pack_lse(lse_all)
 
 
 def attend_kernel(block_rows, key_count, *refs):
@@ -291,11 +288,11 @@
             weight[:, 2 * width + start : 2 * width + stop],
             preferred_element_type=jnp.float32,
         ).astype(jnp.bfloat16)
-    attend_rows(across_query, 0, block_rows, bias[0:1, :], keys, values, across_out)
+    attend_rows(across_query, block_rows, bias[0:1, :], keys, values, across_out)
 
 
 def own_kernel(bias, query, keys, values, out):
-    attend_rows(query, 0, query.shape[0], bias[0:1, :], keys, values, out)
+    attend_rows(query, query.shape[0], bias[0:1, :], keys, values, out)
 
 
 def pack_lse(lse):

time: 37.4 us -> 35.8 us (0.957)
  Pallas kernels: 12.1 us -> 9.46 us
  waiting for transfers between devices: 9.25 us -> 10.2 us
    pallas_call x1, Pallas kernels: 5.53 us -> 4.36 us  [per_device(): pl.pallas_call(functools.partial(attend_kernel, rows, len(key_parts)), ou...]
    pallas_call x1, Pallas kernels: 2.4 us -> 1.4 us  [per_device(): pl.pallas_call(own_kernel, out_shape=shape((rows, width + LANES), jnp.bfl...]
    ppermute x14, waiting for transfers between devices: 9.25 us -> 10.2 us  [swap(): return lax.ppermute(value, 'patch', pairs)]
    pallas_call x1, Pallas kernels: 2.44 us -> 1.99 us  [per_device(): pl.pallas_call(functools.partial(front_kernel, part_index, len(key_masks)...]
  transfers between devices with their start and end apart: 14 -> 14, of which waited for: 6 -> 6; matrix products, arithmetic and copies ran while one was open for 0% -> 0% of each run, Pallas kernels for 7% -> 4%
where the time goes in v2:
time: 35.8 us; the launch traced here: 35.7 us
  starting transfers between devices  15.3 us (43%)
  waiting for transfers between devices  10.2 us (28%)
  Pallas kernels  9.46 us (26%)
  between operations  0.7 us (2%)
    ppermute x14, starting transfers between devices, swap(): return lax.ppermute(value, 'patch', pairs)  15.3 us
    ppermute x14, waiting for transfers between devices, swap(): return lax.ppermute(value, 'patch', pairs)  10.2 us
    pallas_call x1, Pallas kernels, per_device(): pl.pallas_call(functools.partial(attend_kernel, rows, len(key_parts)), ou...  4.36 us
    pallas_call x1, Pallas kernels, per_device(): pl.pallas_call(functools.partial(front_kernel, part_index, len(key_masks)...  1.99 us
    pallas_call x1, Pallas kernels, per_device(): pl.pallas_call(finish_kernel, out_shape=shape((rows, width), jnp.bfloat16...  1.62 us
    pallas_call x1, Pallas kernels, per_device(): pl.pallas_call(own_kernel, out_shape=shape((rows, width + LANES), jnp.bfl...  1.4 us
  transfers between devices with their start and end apart: 14, of which 6 were waited for; matrix products, arithmetic and copies ran while one was open for 0% of the time, Pallas kernels for 4%

profile of v2, /device:TPU:0, one launch (start us, length us, event | category | flops | bytes accessed | tf_op | source)
XLA Modules:
  0.0 35.7 jit_solution(4463616807758442902)
XLA Ops:
  0.7 2.0 %front.1 = (bf16[48,1152]{1,0:T(8,128)(2,1)S(1)}, bf16[8,1152]{1,0:T(8,128)(2,1)S(1)}, f32[48,1152]{1,0:T(8,128)S(1)}, f32[8,384]{1,0:T(8,128)S(1)}, f32[48,128]{1,0:T(8,128)S(1)}) custom-call(s32[1]{0:T(128)S(6)} %copy.11.timestep, s32[16]{0:T(128)} %counts_far.1, bf16[48,1152]{1,0:T(8,128)(2,1)} %tokens_far.1, s32[2,48]{1,0:T(2,128)} %positions_far.1, ...), custom_call_target="tpu_custom_call" | custom-call | tf_op jit(solution)/shard_map/front/pallas_call | solution.py:380
  2.7 0.6 %collective-permute-start = (bf16[8,1152]{1,0:T(8,128)(2,1)S(1)}, bf16[8,1152]{1,0:T(8,128)(2,1)S(1)}, u32[]{:S(2)}, u32[]{:S(2)}) collective-permute-start(bf16[8,1152]{1,0:T(8,128)(2,1)S(1)} %get-tuple-element.15.refs_0_), channel_id=1, source_target_pairs={{0,1},{1,0},{2,3},{3,2},{4,5},{5,4},{6,7},{7,6},{8,9},{9,8},{10,11... | collective-permute-start | bytes 55304 | tf_op jit(solution)/shard_map/ppermute | solution.py:372
  3.2 0.8 %collective-permute-done.refs_1_ = bf16[8,1152]{1,0:T(8,128)(2,1)S(1)} collective-permute-done((bf16[8,1152]{1,0:T(8,128)(2,1)S(1)}, bf16[8,1152]{1,0:T(8,128)(2,1)S(1)}, u32[]{:S(2)}, u32[]{:S(2)}) %collective-permute-start) | collective-permute-done | bytes 18464 | tf_op jit(solution)/shard_map/ppermute | solution.py:372
  4.1 5.0 %collective-permute-start.3 = (bf16[8,1152]{1,0:T(8,128)(2,1)S(1)}, bf16[8,1152]{1,0:T(8,128)(2,1)S(1)}, u32[]{:S(2)}, u32[]{:S(2)}) collective-permute-start(bf16[8,1152]{1,0:T(8,128)(2,1)S(1)} %add.2.refs_0_), channel_id=1, source_target_pairs={{0,12},{1,13},{2,14},{3,15},{4,8},{5,9},{6,10},{7,11},{8,4},{9,5},... | collective-permute-start | bytes 55304 | tf_op jit(solution)/shard_map/ppermute | solution.py:372
  9.1 0.0 collective-permute-start.2
  9.1 0.6 %collective-permute-start.1 = (bf16[8,1152]{1,0:T(8,128)(2,1)S(1)}, bf16[8,1152]{1,0:T(8,128)(2,1)S(1)}, u32[]{:S(2)}, u32[]{:S(2)}) collective-permute-start(bf16[8,1152]{1,0:T(8,128)(2,1)S(1)} %add.2.refs_0_), channel_id=1, source_target_pairs={{0,4},{1,5},{2,6},{3,7},{4,0},{5,1},{6,2},{7,3},{8,12},{9,13},{10,... | collective-permute-start | bytes 55304 | tf_op jit(solution)/shard_map/ppermute | solution.py:372
  9.7 3.7 %collective-permute-start.7 = (bf16[48,1152]{1,0:T(8,128)(2,1)S(1)}, bf16[48,1152]{1,0:T(8,128)(2,1)S(1)}, u32[]{:S(2)}, u32[]{:S(2)}) collective-permute-start(bf16[48,1152]{1,0:T(8,128)(2,1)S(1)} %get-tuple-element.16.refs_3_.refs_11_), channel_id=1, source_target_pairs={{0,12},{1,13},{2,14},{3,15},{4,8},{5,9},{6,10},{7,11},{8,4},{9,5},... | collective-permute-start | bytes 331784 | tf_op jit(solution)/shard_map/ppermute | solution.py:372
  13.5 0.0 collective-permute-start.6
  13.5 0.0 collective-permute-done.3.refs_3_
  13.5 0.6 %collective-permute-start.5 = (bf16[48,1152]{1,0:T(8,128)(2,1)S(1)}, bf16[48,1152]{1,0:T(8,128)(2,1)S(1)}, u32[]{:S(2)}, u32[]{:S(2)}) collective-permute-start(bf16[48,1152]{1,0:T(8,128)(2,1)S(1)} %get-tuple-element.16.refs_3_.refs_11_), channel_id=1, source_target_pairs={{0,4},{1,5},{2,6},{3,7},{4,0},{5,1},{6,2},{7,3},{8,12},{9,13},{10,... | collective-permute-start | bytes 331784 | tf_op jit(solution)/shard_map/ppermute | solution.py:372
  14.1 0.0 collective-permute-done.2.refs_2_
  14.1 0.0 collective-permute-done.1.refs_1_
  14.2 1.7 %collective-permute-start.4 = (bf16[8,1152]{1,0:T(8,128)(2,1)S(1)}, bf16[8,1152]{1,0:T(8,128)(2,1)S(1)}, u32[]{:S(2)}, u32[]{:S(2)}) collective-permute-start(bf16[8,1152]{1,0:T(8,128)(2,1)S(1)} %add.3.refs_1_.sums_a), channel_id=1, source_target_pairs={{0,2},{1,3},{2,0},{3,1},{4,6},{5,7},{6,4},{7,5},{8,10},{9,11},{10,... | collective-permute-start | bytes 55304 | tf_op jit(solution)/shard_map/ppermute | solution.py:372
  15.9 0.4 %collective-permute-start.12 = (bf16[48,1152]{1,0:T(8,128)(2,1)S(1)}, bf16[48,1152]{1,0:T(8,128)(2,1)S(1)}, u32[]{:S(2)}, u32[]{:S(2)}) collective-permute-start(bf16[48,1152]{1,0:T(8,128)(2,1)S(1)} %get-tuple-element.16.refs_3_.refs_11_), channel_id=1, source_target_pairs={{0,2},{1,3},{2,0},{3,1},{4,6},{5,7},{6,4},{7,5},{8,10},{9,11},{10,... | collective-permute-start | bytes 331784 | tf_op jit(solution)/shard_map/ppermute | solution.py:372
  16.3 1.9 %collective-permute-done.4.refs_2_.sums_b = bf16[8,1152]{1,0:T(8,128)(2,1)S(1)} collective-permute-done((bf16[8,1152]{1,0:T(8,128)(2,1)S(1)}, bf16[8,1152]{1,0:T(8,128)(2,1)S(1)}, u32[]{:S(2)}, u32[]{:S(2)}) %collective-permute-start.4) | collective-permute-done | bytes 18464 | tf_op jit(solution)/shard_map/ppermute | solution.py:372
  18.2 0.0 collective-permute-start.8
  18.2 0.0 collective-permute-done.7.refs_6_
  18.2 0.5 %collective-permute-start.11 = (bf16[48,1152]{1,0:T(8,128)(2,1)S(1)}, bf16[48,1152]{1,0:T(8,128)(2,1)S(1)}, u32[]{:S(2)}, u32[]{:S(2)}) collective-permute-start(bf16[48,1152]{1,0:T(8,128)(2,1)S(1)} %collective-permute-done.7.refs_6_), channel_id=1, source_target_pairs={{0,1},{1,0},{2,3},{3,2},{4,5},{5,4},{6,7},{7,6},{8,9},{9,8},{10,11... | collective-permute-start | bytes 331784 | tf_op jit(solution)/shard_map/ppermute | solution.py:372
  18.7 3.8 %collective-permute-done.6.refs_5_ = bf16[48,1152]{1,0:T(8,128)(2,1)S(1)} collective-permute-done((bf16[48,1152]{1,0:T(8,128)(2,1)S(1)}, bf16[48,1152]{1,0:T(8,128)(2,1)S(1)}, u32[]{:S(2)}, u32[]{:S(2)}) %collective-permute-start.6) | collective-permute-done | bytes 110624 | tf_op jit(solution)/shard_map/ppermute | solution.py:372
  22.5 0.0 collective-permute-start.10
  22.5 0.0 collective-permute-done.5.refs_4_
  22.5 0.5 %collective-permute-start.9 = (bf16[48,1152]{1,0:T(8,128)(2,1)S(1)}, bf16[48,1152]{1,0:T(8,128)(2,1)S(1)}, u32[]{:S(2)}, u32[]{:S(2)}) collective-permute-start(bf16[48,1152]{1,0:T(8,128)(2,1)S(1)} %collective-permute-done.5.refs_4_), channel_id=1, source_target_pairs={{0,1},{1,0},{2,3},{3,2},{4,5},{5,4},{6,7},{7,6},{8,9},{9,8},{10,11... | collective-permute-start | bytes 331784 | tf_op jit(solution)/shard_map/ppermute | solution.py:372
  23.1 0.0 collective-permute-done.12.refs_12_
  23.1 0.0 collective-permute-done.8.refs_7_
  23.1 0.0 collective-permute-done.11.refs_10_
  23.1 0.8 %collective-permute-done.10.refs_9_ = bf16[48,1152]{1,0:T(8,128)(2,1)S(1)} collective-permute-done((bf16[48,1152]{1,0:T(8,128)(2,1)S(1)}, bf16[48,1152]{1,0:T(8,128)(2,1)S(1)}, u32[]{:S(2)}, u32[]{:S(2)}) %collective-permute-start.10) | collective-permute-done | bytes 110624 | tf_op jit(solution)/shard_map/ppermute | solution.py:372
  23.9 0.2 collective-permute-done.9.refs_8_
  24.0 4.4 %attend.1 = (bf16[48,1152]{1,0:T(8,128)(2,1)S(1)}, bf16[384,1152]{1,0:T(8,128)(2,1)S(1)}, bf16[384,1152]{1,0:T(8,128)(2,1)S(1)}, bf16[48,1280]{1,0:T(8,128)(2,1)S(1)}) custom-call(f32[8,384]{1,0:T(8,128)S(1)} %get-tuple-element.14.refs_0_.bias, bf16[8,1152]{1,0:T(8,128)(2,1)S(1)} %add.3.refs_1_.sums_a, ...), custom_call_target="tpu_custom_call" | custom-call | tf_op jit(solution)/shard_map/attend/pallas_call | solution.py:433
  28.4 1.6 %collective-permute-start.13 = (bf16[48,1280]{1,0:T(8,128)(2,1)S(1)}, bf16[48,1280]{1,0:T(8,128)(2,1)S(1)}, u32[]{:S(2)}, u32[]{:S(2)}) collective-permute-start(bf16[48,1280]{1,0:T(8,128)(2,1)S(1)} %get-tuple-element.20), channel_id=1, source_target_pairs={{0,2},{1,3},{2,0},{3,1},{4,6},{5,7},{6,4},{7,5},{8,10},{9,11},{10,... | collective-permute-start | bytes 368648 | tf_op jit(solution)/shard_map/ppermute | solution.py:372
  30.0 1.4 %own.1.packed_a = bf16[48,1280]{1,0:T(8,128)(2,1)S(1)} custom-call(f32[8,384]{1,0:T(8,128)S(1)} %get-tuple-element.14.refs_0_.bias, bf16[48,1152]{1,0:T(8,128)(2,1)S(1)} %get-tuple-element.17.query, bf16[384,1152]{1,0:T(8,128)(2,1)S(1)} %get-tuple-element.18.keys, bf16[384,1152]{1,0:T(8,128)(2,1)S(1)} %get-tuple-element.19.values), custom_call_target="tpu_custom_call" | custom-call | flops 17179869184 | bytes 1769472 | tf_op jit(solution)/shard_map/own/pallas_call | solution.py:451
  31.4 2.7 %collective-permute-done.13.packed_b = bf16[48,1280]{1,0:T(8,128)(2,1)S(1)} collective-permute-done((bf16[48,1280]{1,0:T(8,128)(2,1)S(1)}, bf16[48,1280]{1,0:T(8,128)(2,1)S(1)}, u32[]{:S(2)}, u32[]{:S(2)}) %collective-permute-start.13) | collective-permute-done | bytes 122912 | tf_op jit(solution)/shard_map/ppermute | solution.py:372
  34.0 1.6 %finish.1 = bf16[48,1152]{1,0:T(8,128)(2,1)} custom-call(bf16[48,1280]{1,0:T(8,128)(2,1)S(1)} %own.1.packed_a, bf16[48,1280]{1,0:T(8,128)(2,1)S(1)} %collective-permute-done.13.packed_b, f32[48,1152]{1,0:T(8,128)S(1)} %get-tuple-element.21.x_in, f32[48,128]{1,0:T(8,128)S(1)} %get-tuple-element.22.row_valid, bf16[8,1152]{1,0:T(8,128)(2,1)S(1)} %add.3.refs_1_.sums_a, ...), custom_call_target="tpu_custom_call" | custom-call | tf_op jit(solution)/shard_map/finish/pallas_call | solution.py:462
  (9 shorter events, 0.1 us)
Async XLA Ops:
  2.7 1.4 %collective-permute-start = (bf16[8,1152]{1,0:T(8,128)(2,1)S(1)}, bf16[8,1152]{1,0:T(8,128)(2,1)S(1)}, u32[]{:S(2)}, u32[]{:S(2)}) collective-permute-start(bf16[8,1152]{1,0:T(8,128)(2,1)S(1)} %get-tuple-element.15.refs_0_), channel_id=1, source_target_pairs={{0,1},{1,0},{2,3},{3,2},{4,5},{5,4},{6,7},{7,6},{8,9},{9,8},{10,11... | collective-permute-start | bytes 55304 | tf_op jit(solution)/shard_map/ppermute | solution.py:372
  4.1 9.4 %collective-permute-start.3 = (bf16[8,1152]{1,0:T(8,128)(2,1)S(1)}, bf16[8,1152]{1,0:T(8,128)(2,1)S(1)}, u32[]{:S(2)}, u32[]{:S(2)}) collective-permute-start(bf16[8,1152]{1,0:T(8,128)(2,1)S(1)} %add.2.refs_0_), channel_id=1, source_target_pairs={{0,12},{1,13},{2,14},{3,15},{4,8},{5,9},{6,10},{7,11},{8,4},{9,5},... | collective-permute-start | bytes 55304 | tf_op jit(solution)/shard_map/ppermute | solution.py:372
  9.1 5.0 %collective-permute-start.2 = (bf16[8,1152]{1,0:T(8,128)(2,1)S(1)}, bf16[8,1152]{1,0:T(8,128)(2,1)S(1)}, u32[]{:S(2)}, u32[]{:S(2)}) collective-permute-start(bf16[8,1152]{1,0:T(8,128)(2,1)S(1)} %add.2.refs_0_), channel_id=1, source_target_pairs={{0,8},{1,9},{2,10},{3,11},{4,12},{5,13},{6,14},{7,15},{8,0},{9,1},... | collective-permute-start | bytes 55304 | tf_op jit(solution)/shard_map/ppermute | solution.py:372
  9.1 5.0 %collective-permute-start.1 = (bf16[8,1152]{1,0:T(8,128)(2,1)S(1)}, bf16[8,1152]{1,0:T(8,128)(2,1)S(1)}, u32[]{:S(2)}, u32[]{:S(2)}) collective-permute-start(bf16[8,1152]{1,0:T(8,128)(2,1)S(1)} %add.2.refs_0_), channel_id=1, source_target_pairs={{0,4},{1,5},{2,6},{3,7},{4,0},{5,1},{6,2},{7,3},{8,12},{9,13},{10,... | collective-permute-start | bytes 55304 | tf_op jit(solution)/shard_map/ppermute | solution.py:372
  9.7 14.3 %slice-start = ((s8[7962624]{0:T(1024)(128)(4,1)}), s8[4194304]{0:T(1024)(128)(4,1)S(1)}, s32[]{:S(2)}) async-start(s8[7962624]{0:T(1024)(128)(4,1)} %bitcast.1), calls=%async_computation | async-start | bytes 8388608
  9.7 14.3 %slice-start.1 = ((s8[7962624]{0:T(1024)(128)(4,1)}), s8[3768320]{0:T(1024)(128)(4,1)S(1)}, s32[]{:S(2)}) async-start(s8[7962624]{0:T(1024)(128)(4,1)} %bitcast.1), calls=%async_computation.1 | async-start | bytes 7536640
  9.7 8.5 %collective-permute-start.7 = (bf16[48,1152]{1,0:T(8,128)(2,1)S(1)}, bf16[48,1152]{1,0:T(8,128)(2,1)S(1)}, u32[]{:S(2)}, u32[]{:S(2)}) collective-permute-start(bf16[48,1152]{1,0:T(8,128)(2,1)S(1)} %get-tuple-element.16.refs_3_.refs_11_), channel_id=1, source_target_pairs={{0,12},{1,13},{2,14},{3,15},{4,8},{5,9},{6,10},{7,11},{8,4},{9,5},... | collective-permute-start | bytes 331784 | tf_op jit(solution)/shard_map/ppermute | solution.py:372
  13.5 9.1 %collective-permute-start.6 = (bf16[48,1152]{1,0:T(8,128)(2,1)S(1)}, bf16[48,1152]{1,0:T(8,128)(2,1)S(1)}, u32[]{:S(2)}, u32[]{:S(2)}) collective-permute-start(bf16[48,1152]{1,0:T(8,128)(2,1)S(1)} %get-tuple-element.16.refs_3_.refs_11_), channel_id=1, source_target_pairs={{0,8},{1,9},{2,10},{3,11},{4,12},{5,13},{6,14},{7,15},{8,0},{9,1},... | collective-permute-start | bytes 331784 | tf_op jit(solution)/shard_map/ppermute | solution.py:372
  13.5 9.1 %collective-permute-start.5 = (bf16[48,1152]{1,0:T(8,128)(2,1)S(1)}, bf16[48,1152]{1,0:T(8,128)(2,1)S(1)}, u32[]{:S(2)}, u32[]{:S(2)}) collective-permute-start(bf16[48,1152]{1,0:T(8,128)(2,1)S(1)} %get-tuple-element.16.refs_3_.refs_11_), channel_id=1, source_target_pairs={{0,4},{1,5},{2,6},{3,7},{4,0},{5,1},{6,2},{7,3},{8,12},{9,13},{10,... | collective-permute-start | bytes 331784 | tf_op jit(solution)/shard_map/ppermute | solution.py:372
  14.2 4.0 %collective-permute-start.4 = (bf16[8,1152]{1,0:T(8,128)(2,1)S(1)}, bf16[8,1152]{1,0:T(8,128)(2,1)S(1)}, u32[]{:S(2)}, u32[]{:S(2)}) collective-permute-start(bf16[8,1152]{1,0:T(8,128)(2,1)S(1)} %add.3.refs_1_.sums_a), channel_id=1, source_target_pairs={{0,2},{1,3},{2,0},{3,1},{4,6},{5,7},{6,4},{7,5},{8,10},{9,11},{10,... | collective-permute-start | bytes 55304 | tf_op jit(solution)/shard_map/ppermute | solution.py:372
  15.9 7.2 %collective-permute-start.12 = (bf16[48,1152]{1,0:T(8,128)(2,1)S(1)}, bf16[48,1152]{1,0:T(8,128)(2,1)S(1)}, u32[]{:S(2)}, u32[]{:S(2)}) collective-permute-start(bf16[48,1152]{1,0:T(8,128)(2,1)S(1)} %get-tuple-element.16.refs_3_.refs_11_), channel_id=1, source_target_pairs={{0,2},{1,3},{2,0},{3,1},{4,6},{5,7},{6,4},{7,5},{8,10},{9,11},{10,... | collective-permute-start | bytes 331784 | tf_op jit(solution)/shard_map/ppermute | solution.py:372
  18.2 4.9 %collective-permute-start.8 = (bf16[48,1152]{1,0:T(8,128)(2,1)S(1)}, bf16[48,1152]{1,0:T(8,128)(2,1)S(1)}, u32[]{:S(2)}, u32[]{:S(2)}) collective-permute-start(bf16[48,1152]{1,0:T(8,128)(2,1)S(1)} %get-tuple-element.16.refs_3_.refs_11_), channel_id=1, source_target_pairs={{0,1},{1,0},{2,3},{3,2},{4,5},{5,4},{6,7},{7,6},{8,9},{9,8},{10,11... | collective-permute-start | bytes 331784 | tf_op jit(solution)/shard_map/ppermute | solution.py:372
  18.2 4.9 %collective-permute-start.11 = (bf16[48,1152]{1,0:T(8,128)(2,1)S(1)}, bf16[48,1152]{1,0:T(8,128)(2,1)S(1)}, u32[]{:S(2)}, u32[]{:S(2)}) collective-permute-start(bf16[48,1152]{1,0:T(8,128)(2,1)S(1)} %collective-permute-done.7.refs_6_), channel_id=1, source_target_pairs={{0,1},{1,0},{2,3},{3,2},{4,5},{5,4},{6,7},{7,6},{8,9},{9,8},{10,11... | collective-permute-start | bytes 331784 | tf_op jit(solution)/shard_map/ppermute | solution.py:372
  22.5 1.3 %collective-permute-start.10 = (bf16[48,1152]{1,0:T(8,128)(2,1)S(1)}, bf16[48,1152]{1,0:T(8,128)(2,1)S(1)}, u32[]{:S(2)}, u32[]{:S(2)}) collective-permute-start(bf16[48,1152]{1,0:T(8,128)(2,1)S(1)} %collective-permute-done.6.refs_5_), channel_id=1, source_target_pairs={{0,1},{1,0},{2,3},{3,2},{4,5},{5,4},{6,7},{7,6},{8,9},{9,8},{10,11... | collective-permute-start | bytes 331784 | tf_op jit(solution)/shard_map/ppermute | solution.py:372
  22.5 1.5 %collective-permute-start.9 = (bf16[48,1152]{1,0:T(8,128)(2,1)S(1)}, bf16[48,1152]{1,0:T(8,128)(2,1)S(1)}, u32[]{:S(2)}, u32[]{:S(2)}) collective-permute-start(bf16[48,1152]{1,0:T(8,128)(2,1)S(1)} %collective-permute-done.5.refs_4_), channel_id=1, source_target_pairs={{0,1},{1,0},{2,3},{3,2},{4,5},{5,4},{6,7},{7,6},{8,9},{9,8},{10,11... | collective-permute-start | bytes 331784 | tf_op jit(solution)/shard_map/ppermute | solution.py:372
  28.4 5.6 %collective-permute-start.13 = (bf16[48,1280]{1,0:T(8,128)(2,1)S(1)}, bf16[48,1280]{1,0:T(8,128)(2,1)S(1)}, u32[]{:S(2)}, u32[]{:S(2)}) collective-permute-start(bf16[48,1280]{1,0:T(8,128)(2,1)S(1)} %get-tuple-element.20), channel_id=1, source_target_pairs={{0,2},{1,3},{2,0},{3,1},{4,6},{5,7},{6,4},{7,5},{8,10},{9,11},{10,... | collective-permute-start | bytes 368648 | tf_op jit(solution)/shard_map/ppermute | solution.py:372
  30.0 4.1 %copy-start = (bf16[1152,1152]{1,0:T(8,128)(2,1)S(1)}, bf16[1152,1152]{1,0:T(8,128)(2,1)}, u32[]{:S(2)}) copy-start(bf16[1152,1152]{1,0:T(8,128)(2,1)} %weight.1) | copy-start | bytes 7962628

commit v3 on v2

--- a/solution.py
+++ b/solution.py
@@ -12,6 +12,7 @@
 
 HEADS = 16
 LANES = 128
+PIECE = 768
 SUM_ROWS = 8
 CORE_MASK = 1
 MERGE_MASK = 2
@@ -94,10 +95,10 @@
     order = (
         (table_far, table),
         (positions_far, positions),
+        (tokens_far, tokens),
         (time_in_far, time_in),
         (time_out_far, time_out),
         (ada_weight_far, ada_weight),
-        (tokens_far, tokens),
         (counts_far, counts),
     )
     copies = [
@@ -108,7 +109,7 @@
         copy.start()
     rows, width = tokens.shape
     freq_size = time_in.shape[0]
-    for copy in copies[:2]:
+    for copy in copies[:3]:
         copy.wait()
     place = positions[...].astype(jnp.float32)
     same = lax.broadcasted_iota(jnp.int32, (rows, rows), 0) == lax.broadcasted_iota(
@@ -118,14 +119,18 @@
         jnp.sum(jnp.where(same, place[axis : axis + 1, :], 0.0), axis=1, keepdims=True)
         for axis in range(2)
     ]
-    where_to = jnp.where(table[2:3, :] > 0.5, column[1], column[0])
-    embed = sine(where_to * table[0:1, :], table[1:2, :])
+    for start in range(0, rows, SUM_ROWS):
+        chunk = slice(start, start + SUM_ROWS)
+        where_to = jnp.where(table[2:3, :] > 0.5, column[1][chunk, :], column[0][chunk, :])
+        x_in_ref[chunk, :] = tokens[chunk, :].astype(jnp.float32) + sine(
+            where_to * table[0:1, :], jnp.broadcast_to(table[1:2, :], where_to.shape)
+        )
     angle = timestep[0].astype(jnp.float32) * jnp.broadcast_to(
         table[3:4, :freq_size], (SUM_ROWS, freq_size)
     )
     shifted = jnp.broadcast_to(table[4:5, :freq_size], (SUM_ROWS, freq_size))
     features = sine(angle, shifted).astype(jnp.bfloat16)
-    for copy in copies[2:]:
+    for copy in copies[3:]:
         copy.wait()
     hidden = silu(jnp.dot(features, time_in[...], preferred_element_type=jnp.float32))
     cond = lax.dot_general(
@@ -137,11 +142,10 @@
     partial = jnp.dot(
         silu(cond).astype(jnp.bfloat16), ada_weight[...], preferred_element_type=jnp.float32
     )
-    x_in = tokens[...].astype(jnp.float32) + embed
+    x_in = x_in_ref[...]
     centered = x_in - jnp.mean(x_in, axis=1, keepdims=True)
     variance = jnp.mean(centered * centered, axis=1, keepdims=True)
     message[...] = (centered * lax.rsqrt(variance + 1e-06)).astype(jnp.bfloat16)
-    x_in_ref[...] = x_in
     sums[...] = pack_sums([partial[:, piece * width : (piece + 1) * width] for piece in range(3)])
 
     my_index = lax.axis_index("patch")
@@ -272,27 +276,36 @@
             place += block_rows
     mod_queries[:block_rows, :] = modulate(own[...])
     mod_queries[block_rows:, :] = modulate(across[...])
-    piece = 3 * LANES
-    for start in range(0, width, piece):
-        stop = min(start + piece, width)
+    for start in range(0, width, PIECE):
+        stop = min(start + PIECE, width)
         both = jnp.dot(
             mod_queries[...], weight[:, start:stop], preferred_element_type=jnp.float32
         ).astype(jnp.bfloat16)
         own_query[:, start:stop] = both[:block_rows, :]
         across_query[:, start:stop] = both[block_rows:, :]
-        keys[:, start:stop] = jnp.dot(
+    for start in range(0, 2 * width, PIECE):
+        stop = min(start + PIECE, 2 * width)
+        both = jnp.dot(
             mod_keys[...], weight[:, width + start : width + stop], preferred_element_type=jnp.float32
         ).astype(jnp.bfloat16)
-        values[:, start:stop] = jnp.dot(
-            mod_keys[...],
-            weight[:, 2 * width + start : 2 * width + stop],
-            preferred_element_type=jnp.float32,
-        ).astype(jnp.bfloat16)
+        split = min(max(width - start, 0), stop - start)
+        if split:
+            keys[:, start : start + split] = both[:, :split]
+        if split < stop - start:
+            values[:, start + split - width : stop - width] = both[:, split:]
     attend_rows(across_query, block_rows, bias[0:1, :], keys, values, across_out)
 
 
-def own_kernel(bias, query, keys, values, out):
+def own_kernel(bias, query, keys, values, out, lse, expand):
+    width = query.shape[1]
+    head_size = width // HEADS
     attend_rows(query, query.shape[0], bias[0:1, :], keys, values, out)
+    lse[...] = unpack_lse(out[:, width:])
+    head_id = lax.broadcasted_iota(jnp.int32, expand.shape, 0)
+    lane_id = lax.broadcasted_iota(jnp.int32, expand.shape, 1)
+    low = head_id * head_size
+    inside = jnp.logical_and(lane_id >= low, lane_id < low + head_size)
+    expand[...] = inside.astype(jnp.float32).astype(jnp.bfloat16)
 
 
 def pack_lse(lse):
@@ -314,33 +327,24 @@
     return jnp.dot(packed, chosen, preferred_element_type=jnp.float32)
 
 
-def spread(value, width):
-    head_size = width // HEADS
-    head_id = lax.broadcasted_iota(jnp.int32, (LANES, width), 0)
-    lane_id = lax.broadcasted_iota(jnp.int32, (LANES, width), 1)
-    low = head_id * head_size
-    expand = jnp.logical_and(lane_id >= low, lane_id < low + head_size).astype(jnp.bfloat16)
-    high, rest = high_low(value)
-    return jnp.dot(high, expand, preferred_element_type=jnp.float32) + jnp.dot(
-        rest, expand, preferred_element_type=jnp.float32
-    )
-
-
-def merge(packed_a, packed_b):
-    width = packed_a.shape[1] - LANES
-    lse_a, lse_b = unpack_lse(packed_a[:, width:]), unpack_lse(packed_b[:, width:])
+def merge(value_a, lse_a, packed_b, expand):
+    width = value_a.shape[1] - LANES
+    lse_b = unpack_lse(packed_b[:, width:])
     top = jnp.maximum(lse_a, lse_b)
     part_a = jnp.exp2(lse_a - top)
     part_b = jnp.exp2(lse_b - top)
-    total = part_a + part_b
-    share = spread(part_b / total, width)
-    first = packed_a[:, :width].astype(jnp.float32)
-    value = first + share * (packed_b[:, :width].astype(jnp.float32) - first)
-    return value
-
-
-def finish_kernel(packed_a, packed_b, x_in, row_valid, sums_a, sums_b, weight, out):
-    value = merge(packed_a[...], packed_b[...])
+    high, rest = high_low(part_b / (part_a + part_b))
+    share = jnp.dot(high, expand, preferred_element_type=jnp.float32) + jnp.dot(
+        rest, expand, preferred_element_type=jnp.float32
+    )
+    first = value_a[:, :width].astype(jnp.float32)
+    return first + share * (packed_b[:, :width].astype(jnp.float32) - first)
+
+
+def finish_kernel(
+    value_a, lse_a, expand, packed_b, x_in, row_valid, sums_a, sums_b, weight, out
+):
+    value = merge(value_a[...], lse_a[...], packed_b[...], expand[...])
     gate = sum_piece(sums_a[...].astype(jnp.float32) + sums_b[...].astype(jnp.float32), 2)
     projected = jnp.dot(
         value.astype(jnp.bfloat16), weight[...], preferred_element_type=jnp.float32
@@ -448,11 +452,15 @@
         compiler_params=grant(ATTEND_GRANT if direct else 56),
         name="attend",
     )(bias, half_sums, other_sums, *key_parts, message, across, qkv_weight)
-    own = pl.pallas_call(
+    own, own_lse, expand = pl.pallas_call(
         own_kernel,
-        out_shape=shape((rows, width + LANES), jnp.bfloat16),
+        out_shape=(
+            shape((rows, width + LANES), jnp.bfloat16),
+            shape((rows, LANES), jnp.float32),
+            shape((LANES, width), jnp.bfloat16),
+        ),
         in_specs=[vmem()] * 4,
-        out_specs=vmem(),
+        out_specs=(vmem(),) * 3,
         compiler_params=grant(8 if direct else 40),
         cost_estimate=pl.CostEstimate(
             flops=1 << 34, bytes_accessed=4 * keys.size, transcendentals=0
@@ -462,11 +470,21 @@
     return pl.pallas_call(
         finish_kernel,
         out_shape=shape((rows, width), jnp.bfloat16),
-        in_specs=[vmem()] * 7,
+        in_specs=[vmem()] * 9,
         out_specs=vmem(),
         compiler_params=grant(8),
         name="finish",
-    )(own, swap(send, MERGE_MASK), x_in, row_valid, half_sums, other_sums, out_weight)
+    )(
+        own,
+        own_lse,
+        expand,
+        swap(send, MERGE_MASK),
+        x_in,
+        row_valid,
+        half_sums,
+        other_sums,
+        out_weight,
+    )
 
 
 def solution(mesh):

time: 35.8 us -> 35.6 us (level)
  transfers between devices with their start and end apart: 14 -> 14, of which waited for: 6 -> 6; matrix products, arithmetic and copies ran while one was open for 0% -> 0% of each run, Pallas kernels for 4% -> 5%
where the time goes in v3:
time: 35.6 us; the launch traced here: 35.4 us
  starting transfers between devices  15.2 us (43%)
  waiting for transfers between devices  10 us (28%)
  Pallas kernels  9.46 us (27%)
  between operations  0.69 us (2%)
    ppermute x14, starting transfers between devices, swap(): return lax.ppermute(value, 'patch', pairs)  15.2 us
    ppermute x14, waiting for transfers between devices, swap(): return lax.ppermute(value, 'patch', pairs)  10 us
    pallas_call x1, Pallas kernels, per_device(): pl.pallas_call(functools.partial(attend_kernel, rows, len(key_parts)), ou...  4.14 us
    pallas_call x1, Pallas kernels, per_device(): pl.pallas_call(functools.partial(front_kernel, part_index, len(key_masks)...  2.03 us
    pallas_call x1, Pallas kernels, per_device(): pl.pallas_call(own_kernel, out_shape=(shape((rows, width + LANES), jnp.bf...  1.63 us
    pallas_call x1, Pallas kernels, per_device(): pl.pallas_call(finish_kernel, out_shape=shape((rows, width), jnp.bfloat16...  1.57 us
  transfers between devices with their start and end apart: 14, of which 6 were waited for; matrix products, arithmetic and copies ran while one was open for 0% of the time, Pallas kernels for 5%

profile of v3, /device:TPU:0, one launch (start us, length us, event | category | flops | bytes accessed | tf_op | source)
XLA Modules:
  0.0 35.4 jit_solution(12057714556196704441)
XLA Ops:
  0.7 2.0 %front.1 = (bf16[48,1152]{1,0:T(8,128)(2,1)S(1)}, bf16[8,1152]{1,0:T(8,128)(2,1)S(1)}, f32[48,1152]{1,0:T(8,128)S(1)}, f32[8,384]{1,0:T(8,128)S(1)}, f32[48,128]{1,0:T(8,128)S(1)}) custom-call(s32[1]{0:T(128)S(6)} %copy.11.timestep, s32[16]{0:T(128)} %counts_far.1, bf16[48,1152]{1,0:T(8,128)(2,1)} %tokens_far.1, s32[2,48]{1,0:T(2,128)} %positions_far.1, ...), custom_call_target="tpu_custom_call" | custom-call | tf_op jit(solution)/shard_map/front/pallas_call | solution.py:384
  2.7 0.6 %collective-permute-start = (bf16[8,1152]{1,0:T(8,128)(2,1)S(1)}, bf16[8,1152]{1,0:T(8,128)(2,1)S(1)}, u32[]{:S(2)}, u32[]{:S(2)}) collective-permute-start(bf16[8,1152]{1,0:T(8,128)(2,1)S(1)} %get-tuple-element.18.refs_0_), channel_id=1, source_target_pairs={{0,1},{1,0},{2,3},{3,2},{4,5},{5,4},{6,7},{7,6},{8,9},{9,8},{10,11... | collective-permute-start | bytes 55304 | tf_op jit(solution)/shard_map/ppermute | solution.py:376
  3.3 0.8 %collective-permute-done.refs_1_ = bf16[8,1152]{1,0:T(8,128)(2,1)S(1)} collective-permute-done((bf16[8,1152]{1,0:T(8,128)(2,1)S(1)}, bf16[8,1152]{1,0:T(8,128)(2,1)S(1)}, u32[]{:S(2)}, u32[]{:S(2)}) %collective-permute-start) | collective-permute-done | bytes 18464 | tf_op jit(solution)/shard_map/ppermute | solution.py:376
  4.1 5.0 %collective-permute-start.3 = (bf16[8,1152]{1,0:T(8,128)(2,1)S(1)}, bf16[8,1152]{1,0:T(8,128)(2,1)S(1)}, u32[]{:S(2)}, u32[]{:S(2)}) collective-permute-start(bf16[8,1152]{1,0:T(8,128)(2,1)S(1)} %add.2.refs_0_), channel_id=1, source_target_pairs={{0,12},{1,13},{2,14},{3,15},{4,8},{5,9},{6,10},{7,11},{8,4},{9,5},... | collective-permute-start | bytes 55304 | tf_op jit(solution)/shard_map/ppermute | solution.py:376
  9.1 0.0 collective-permute-start.2
  9.1 0.6 %collective-permute-start.1 = (bf16[8,1152]{1,0:T(8,128)(2,1)S(1)}, bf16[8,1152]{1,0:T(8,128)(2,1)S(1)}, u32[]{:S(2)}, u32[]{:S(2)}) collective-permute-start(bf16[8,1152]{1,0:T(8,128)(2,1)S(1)} %add.2.refs_0_), channel_id=1, source_target_pairs={{0,4},{1,5},{2,6},{3,7},{4,0},{5,1},{6,2},{7,3},{8,12},{9,13},{10,... | collective-permute-start | bytes 55304 | tf_op jit(solution)/shard_map/ppermute | solution.py:376
  9.8 3.7 %collective-permute-start.7 = (bf16[48,1152]{1,0:T(8,128)(2,1)S(1)}, bf16[48,1152]{1,0:T(8,128)(2,1)S(1)}, u32[]{:S(2)}, u32[]{:S(2)}) collective-permute-start(bf16[48,1152]{1,0:T(8,128)(2,1)S(1)} %get-tuple-element.19.refs_3_.refs_11_), channel_id=1, source_target_pairs={{0,12},{1,13},{2,14},{3,15},{4,8},{5,9},{6,10},{7,11},{8,4},{9,5},... | collective-permute-start | bytes 331784 | tf_op jit(solution)/shard_map/ppermute | solution.py:376
  13.5 0.0 collective-permute-start.6
  13.5 0.0 collective-permute-done.3.refs_3_
  13.5 0.6 %collective-permute-start.5 = (bf16[48,1152]{1,0:T(8,128)(2,1)S(1)}, bf16[48,1152]{1,0:T(8,128)(2,1)S(1)}, u32[]{:S(2)}, u32[]{:S(2)}) collective-permute-start(bf16[48,1152]{1,0:T(8,128)(2,1)S(1)} %get-tuple-element.19.refs_3_.refs_11_), channel_id=1, source_target_pairs={{0,4},{1,5},{2,6},{3,7},{4,0},{5,1},{6,2},{7,3},{8,12},{9,13},{10,... | collective-permute-start | bytes 331784 | tf_op jit(solution)/shard_map/ppermute | solution.py:376
  14.2 0.0 collective-permute-done.2.refs_2_
  14.2 0.0 collective-permute-done.1.refs_1_
  14.2 1.7 %collective-permute-start.4 = (bf16[8,1152]{1,0:T(8,128)(2,1)S(1)}, bf16[8,1152]{1,0:T(8,128)(2,1)S(1)}, u32[]{:S(2)}, u32[]{:S(2)}) collective-permute-start(bf16[8,1152]{1,0:T(8,128)(2,1)S(1)} %add.3.refs_1_.sums_a), channel_id=1, source_target_pairs={{0,2},{1,3},{2,0},{3,1},{4,6},{5,7},{6,4},{7,5},{8,10},{9,11},{10,... | collective-permute-start | bytes 55304 | tf_op jit(solution)/shard_map/ppermute | solution.py:376
  15.9 0.4 %collective-permute-start.12 = (bf16[48,1152]{1,0:T(8,128)(2,1)S(1)}, bf16[48,1152]{1,0:T(8,128)(2,1)S(1)}, u32[]{:S(2)}, u32[]{:S(2)}) collective-permute-start(bf16[48,1152]{1,0:T(8,128)(2,1)S(1)} %get-tuple-element.19.refs_3_.refs_11_), channel_id=1, source_target_pairs={{0,2},{1,3},{2,0},{3,1},{4,6},{5,7},{6,4},{7,5},{8,10},{9,11},{10,... | collective-permute-start | bytes 331784 | tf_op jit(solution)/shard_map/ppermute | solution.py:376
  16.3 1.9 %collective-permute-done.4.refs_2_.sums_b = bf16[8,1152]{1,0:T(8,128)(2,1)S(1)} collective-permute-done((bf16[8,1152]{1,0:T(8,128)(2,1)S(1)}, bf16[8,1152]{1,0:T(8,128)(2,1)S(1)}, u32[]{:S(2)}, u32[]{:S(2)}) %collective-permute-start.4) | collective-permute-done | bytes 18464 | tf_op jit(solution)/shard_map/ppermute | solution.py:376
  18.2 0.0 collective-permute-start.8
  18.2 0.0 collective-permute-done.7.refs_6_
  18.2 0.5 %collective-permute-start.11 = (bf16[48,1152]{1,0:T(8,128)(2,1)S(1)}, bf16[48,1152]{1,0:T(8,128)(2,1)S(1)}, u32[]{:S(2)}, u32[]{:S(2)}) collective-permute-start(bf16[48,1152]{1,0:T(8,128)(2,1)S(1)} %collective-permute-done.7.refs_6_), channel_id=1, source_target_pairs={{0,1},{1,0},{2,3},{3,2},{4,5},{5,4},{6,7},{7,6},{8,9},{9,8},{10,11... | collective-permute-start | bytes 331784 | tf_op jit(solution)/shard_map/ppermute | solution.py:376
  18.8 3.8 %collective-permute-done.6.refs_5_ = bf16[48,1152]{1,0:T(8,128)(2,1)S(1)} collective-permute-done((bf16[48,1152]{1,0:T(8,128)(2,1)S(1)}, bf16[48,1152]{1,0:T(8,128)(2,1)S(1)}, u32[]{:S(2)}, u32[]{:S(2)}) %collective-permute-start.6) | collective-permute-done | bytes 110624 | tf_op jit(solution)/shard_map/ppermute | solution.py:376
  22.6 0.0 collective-permute-start.10
  22.6 0.0 collective-permute-done.5.refs_4_
  22.6 0.5 %collective-permute-start.9 = (bf16[48,1152]{1,0:T(8,128)(2,1)S(1)}, bf16[48,1152]{1,0:T(8,128)(2,1)S(1)}, u32[]{:S(2)}, u32[]{:S(2)}) collective-permute-start(bf16[48,1152]{1,0:T(8,128)(2,1)S(1)} %collective-permute-done.5.refs_4_), channel_id=1, source_target_pairs={{0,1},{1,0},{2,3},{3,2},{4,5},{5,4},{6,7},{7,6},{8,9},{9,8},{10,11... | collective-permute-start | bytes 331784 | tf_op jit(solution)/shard_map/ppermute | solution.py:376
  23.1 0.0 collective-permute-done.12.refs_12_
  23.1 0.0 collective-permute-done.8.refs_7_
  23.1 0.0 collective-permute-done.11.refs_10_
  23.1 0.8 %collective-permute-done.10.refs_9_ = bf16[48,1152]{1,0:T(8,128)(2,1)S(1)} collective-permute-done((bf16[48,1152]{1,0:T(8,128)(2,1)S(1)}, bf16[48,1152]{1,0:T(8,128)(2,1)S(1)}, u32[]{:S(2)}, u32[]{:S(2)}) %collective-permute-start.10) | collective-permute-done | bytes 110624 | tf_op jit(solution)/shard_map/ppermute | solution.py:376
  23.9 0.2 collective-permute-done.9.refs_8_
  24.1 4.1 %attend.1 = (bf16[48,1152]{1,0:T(8,128)(2,1)S(1)}, bf16[384,1152]{1,0:T(8,128)(2,1)S(1)}, bf16[384,1152]{1,0:T(8,128)(2,1)S(1)}, bf16[48,1280]{1,0:T(8,128)(2,1)S(1)}) custom-call(f32[8,384]{1,0:T(8,128)S(1)} %get-tuple-element.17.refs_0_.bias, bf16[8,1152]{1,0:T(8,128)(2,1)S(1)} %add.3.refs_1_.sums_a, ...), custom_call_target="tpu_custom_call" | custom-call | tf_op jit(solution)/shard_map/attend/pallas_call | solution.py:437
  28.2 1.6 %collective-permute-start.13 = (bf16[48,1280]{1,0:T(8,128)(2,1)S(1)}, bf16[48,1280]{1,0:T(8,128)(2,1)S(1)}, u32[]{:S(2)}, u32[]{:S(2)}) collective-permute-start(bf16[48,1280]{1,0:T(8,128)(2,1)S(1)} %get-tuple-element.26), channel_id=1, source_target_pairs={{0,2},{1,3},{2,0},{3,1},{4,6},{5,7},{6,4},{7,5},{8,10},{9,11},{10,... | collective-permute-start | bytes 368648 | tf_op jit(solution)/shard_map/ppermute | solution.py:376
  29.8 1.6 %own.1 = (bf16[48,1280]{1,0:T(8,128)(2,1)S(1)}, f32[48,128]{1,0:T(8,128)S(1)}, bf16[128,1152]{1,0:T(8,128)(2,1)S(1)}) custom-call(f32[8,384]{1,0:T(8,128)S(1)} %get-tuple-element.17.refs_0_.bias, bf16[48,1152]{1,0:T(8,128)(2,1)S(1)} %get-tuple-element.20.query, bf16[384,1152]{1,0:T(8,128)(2,1)S(1)} %get-tuple-element.21.keys, ...), custom_call_target="tpu_custom_call" | custom-call | flops 17179869184 | bytes 1769472 | tf_op jit(solution)/shard_map/own/pallas_call | solution.py:455
  31.4 2.5 %collective-permute-done.13.packed_b = bf16[48,1280]{1,0:T(8,128)(2,1)S(1)} collective-permute-done((bf16[48,1280]{1,0:T(8,128)(2,1)S(1)}, bf16[48,1280]{1,0:T(8,128)(2,1)S(1)}, u32[]{:S(2)}, u32[]{:S(2)}) %collective-permute-start.13) | collective-permute-done | bytes 122912 | tf_op jit(solution)/shard_map/ppermute | solution.py:376
  33.9 1.6 %finish.1 = bf16[48,1152]{1,0:T(8,128)(2,1)} custom-call(bf16[48,1280]{1,0:T(8,128)(2,1)S(1)} %get-tuple-element.23.value_a, f32[48,128]{1,0:T(8,128)S(1)} %get-tuple-element.24.lse_a, bf16[128,1152]{1,0:T(8,128)(2,1)S(1)} %get-tuple-element.25.expand, bf16[48,1280]{1,0:T(8,128)(2,1)S(1)} %collective-permute-done.13.packed_b, ...), custom_call_target="tpu_custom_call" | custom-call | tf_op jit(solution)/shard_map/finish/pallas_call | solution.py:470
  (9 shorter events, 0.1 us)
Async XLA Ops:
  2.7 1.4 %collective-permute-start = (bf16[8,1152]{1,0:T(8,128)(2,1)S(1)}, bf16[8,1152]{1,0:T(8,128)(2,1)S(1)}, u32[]{:S(2)}, u32[]{:S(2)}) collective-permute-start(bf16[8,1152]{1,0:T(8,128)(2,1)S(1)} %get-tuple-element.18.refs_0_), channel_id=1, source_target_pairs={{0,1},{1,0},{2,3},{3,2},{4,5},{5,4},{6,7},{7,6},{8,9},{9,8},{10,11... | collective-permute-start | bytes 55304 | tf_op jit(solution)/shard_map/ppermute | solution.py:376
  4.1 9.4 %collective-permute-start.3 = (bf16[8,1152]{1,0:T(8,128)(2,1)S(1)}, bf16[8,1152]{1,0:T(8,128)(2,1)S(1)}, u32[]{:S(2)}, u32[]{:S(2)}) collective-permute-start(bf16[8,1152]{1,0:T(8,128)(2,1)S(1)} %add.2.refs_0_), channel_id=1, source_target_pairs={{0,12},{1,13},{2,14},{3,15},{4,8},{5,9},{6,10},{7,11},{8,4},{9,5},... | collective-permute-start | bytes 55304 | tf_op jit(solution)/shard_map/ppermute | solution.py:376
  9.1 5.0 %collective-permute-start.2 = (bf16[8,1152]{1,0:T(8,128)(2,1)S(1)}, bf16[8,1152]{1,0:T(8,128)(2,1)S(1)}, u32[]{:S(2)}, u32[]{:S(2)}) collective-permute-start(bf16[8,1152]{1,0:T(8,128)(2,1)S(1)} %add.2.refs_0_), channel_id=1, source_target_pairs={{0,8},{1,9},{2,10},{3,11},{4,12},{5,13},{6,14},{7,15},{8,0},{9,1},... | collective-permute-start | bytes 55304 | tf_op jit(solution)/shard_map/ppermute | solution.py:376
  9.1 5.0 %collective-permute-start.1 = (bf16[8,1152]{1,0:T(8,128)(2,1)S(1)}, bf16[8,1152]{1,0:T(8,128)(2,1)S(1)}, u32[]{:S(2)}, u32[]{:S(2)}) collective-permute-start(bf16[8,1152]{1,0:T(8,128)(2,1)S(1)} %add.2.refs_0_), channel_id=1, source_target_pairs={{0,4},{1,5},{2,6},{3,7},{4,0},{5,1},{6,2},{7,3},{8,12},{9,13},{10,... | collective-permute-start | bytes 55304 | tf_op jit(solution)/shard_map/ppermute | solution.py:376
  9.8 14.3 %slice-start = ((s8[7962624]{0:T(1024)(128)(4,1)}), s8[4194304]{0:T(1024)(128)(4,1)S(1)}, s32[]{:S(2)}) async-start(s8[7962624]{0:T(1024)(128)(4,1)} %bitcast.1), calls=%async_computation | async-start | bytes 8388608
  9.8 14.3 %slice-start.1 = ((s8[7962624]{0:T(1024)(128)(4,1)}), s8[3768320]{0:T(1024)(128)(4,1)S(1)}, s32[]{:S(2)}) async-start(s8[7962624]{0:T(1024)(128)(4,1)} %bitcast.1), calls=%async_computation.1 | async-start | bytes 7536640
  9.8 8.5 %collective-permute-start.7 = (bf16[48,1152]{1,0:T(8,128)(2,1)S(1)}, bf16[48,1152]{1,0:T(8,128)(2,1)S(1)}, u32[]{:S(2)}, u32[]{:S(2)}) collective-permute-start(bf16[48,1152]{1,0:T(8,128)(2,1)S(1)} %get-tuple-element.19.refs_3_.refs_11_), channel_id=1, source_target_pairs={{0,12},{1,13},{2,14},{3,15},{4,8},{5,9},{6,10},{7,11},{8,4},{9,5},... | collective-permute-start | bytes 331784 | tf_op jit(solution)/shard_map/ppermute | solution.py:376
  13.5 9.1 %collective-permute-start.6 = (bf16[48,1152]{1,0:T(8,128)(2,1)S(1)}, bf16[48,1152]{1,0:T(8,128)(2,1)S(1)}, u32[]{:S(2)}, u32[]{:S(2)}) collective-permute-start(bf16[48,1152]{1,0:T(8,128)(2,1)S(1)} %get-tuple-element.19.refs_3_.refs_11_), channel_id=1, source_target_pairs={{0,8},{1,9},{2,10},{3,11},{4,12},{5,13},{6,14},{7,15},{8,0},{9,1},... | collective-permute-start | bytes 331784 | tf_op jit(solution)/shard_map/ppermute | solution.py:376
  13.5 9.1 %collective-permute-start.5 = (bf16[48,1152]{1,0:T(8,128)(2,1)S(1)}, bf16[48,1152]{1,0:T(8,128)(2,1)S(1)}, u32[]{:S(2)}, u32[]{:S(2)}) collective-permute-start(bf16[48,1152]{1,0:T(8,128)(2,1)S(1)} %get-tuple-element.19.refs_3_.refs_11_), channel_id=1, source_target_pairs={{0,4},{1,5},{2,6},{3,7},{4,0},{5,1},{6,2},{7,3},{8,12},{9,13},{10,... | collective-permute-start | bytes 331784 | tf_op jit(solution)/shard_map/ppermute | solution.py:376
  14.2 4.0 %collective-permute-start.4 = (bf16[8,1152]{1,0:T(8,128)(2,1)S(1)}, bf16[8,1152]{1,0:T(8,128)(2,1)S(1)}, u32[]{:S(2)}, u32[]{:S(2)}) collective-permute-start(bf16[8,1152]{1,0:T(8,128)(2,1)S(1)} %add.3.refs_1_.sums_a), channel_id=1, source_target_pairs={{0,2},{1,3},{2,0},{3,1},{4,6},{5,7},{6,4},{7,5},{8,10},{9,11},{10,... | collective-permute-start | bytes 55304 | tf_op jit(solution)/shard_map/ppermute | solution.py:376
  15.9 7.2 %collective-permute-start.12 = (bf16[48,1152]{1,0:T(8,128)(2,1)S(1)}, bf16[48,1152]{1,0:T(8,128)(2,1)S(1)}, u32[]{:S(2)}, u32[]{:S(2)}) collective-permute-start(bf16[48,1152]{1,0:T(8,128)(2,1)S(1)} %get-tuple-element.19.refs_3_.refs_11_), channel_id=1, source_target_pairs={{0,2},{1,3},{2,0},{3,1},{4,6},{5,7},{6,4},{7,5},{8,10},{9,11},{10,... | collective-permute-start | bytes 331784 | tf_op jit(solution)/shard_map/ppermute | solution.py:376
  18.2 4.9 %collective-permute-start.8 = (bf16[48,1152]{1,0:T(8,128)(2,1)S(1)}, bf16[48,1152]{1,0:T(8,128)(2,1)S(1)}, u32[]{:S(2)}, u32[]{:S(2)}) collective-permute-start(bf16[48,1152]{1,0:T(8,128)(2,1)S(1)} %get-tuple-element.19.refs_3_.refs_11_), channel_id=1, source_target_pairs={{0,1},{1,0},{2,3},{3,2},{4,5},{5,4},{6,7},{7,6},{8,9},{9,8},{10,11... | collective-permute-start | bytes 331784 | tf_op jit(solution)/shard_map/ppermute | solution.py:376
  18.2 4.9 %collective-permute-start.11 = (bf16[48,1152]{1,0:T(8,128)(2,1)S(1)}, bf16[48,1152]{1,0:T(8,128)(2,1)S(1)}, u32[]{:S(2)}, u32[]{:S(2)}) collective-permute-start(bf16[48,1152]{1,0:T(8,128)(2,1)S(1)} %collective-permute-done.7.refs_6_), channel_id=1, source_target_pairs={{0,1},{1,0},{2,3},{3,2},{4,5},{5,4},{6,7},{7,6},{8,9},{9,8},{10,11... | collective-permute-start | bytes 331784 | tf_op jit(solution)/shard_map/ppermute | solution.py:376
  22.6 1.3 %collective-permute-start.10 = (bf16[48,1152]{1,0:T(8,128)(2,1)S(1)}, bf16[48,1152]{1,0:T(8,128)(2,1)S(1)}, u32[]{:S(2)}, u32[]{:S(2)}) collective-permute-start(bf16[48,1152]{1,0:T(8,128)(2,1)S(1)} %collective-permute-done.6.refs_5_), channel_id=1, source_target_pairs={{0,1},{1,0},{2,3},{3,2},{4,5},{5,4},{6,7},{7,6},{8,9},{9,8},{10,11... | collective-permute-start | bytes 331784 | tf_op jit(solution)/shard_map/ppermute | solution.py:376
  22.6 1.5 %collective-permute-start.9 = (bf16[48,1152]{1,0:T(8,128)(2,1)S(1)}, bf16[48,1152]{1,0:T(8,128)(2,1)S(1)}, u32[]{:S(2)}, u32[]{:S(2)}) collective-permute-start(bf16[48,1152]{1,0:T(8,128)(2,1)S(1)} %collective-permute-done.5.refs_4_), channel_id=1, source_target_pairs={{0,1},{1,0},{2,3},{3,2},{4,5},{5,4},{6,7},{7,6},{8,9},{9,8},{10,11... | collective-permute-start | bytes 331784 | tf_op jit(solution)/shard_map/ppermute | solution.py:376
  28.2 5.6 %collective-permute-start.13 = (bf16[48,1280]{1,0:T(8,128)(2,1)S(1)}, bf16[48,1280]{1,0:T(8,128)(2,1)S(1)}, u32[]{:S(2)}, u32[]{:S(2)}) collective-permute-start(bf16[48,1280]{1,0:T(8,128)(2,1)S(1)} %get-tuple-element.26), channel_id=1, source_target_pairs={{0,2},{1,3},{2,0},{3,1},{4,6},{5,7},{6,4},{7,5},{8,10},{9,11},{10,... | collective-permute-start | bytes 368648 | tf_op jit(solution)/shard_map/ppermute | solution.py:376
  29.8 4.1 %copy-start = (bf16[1152,1152]{1,0:T(8,128)(2,1)S(1)}, bf16[1152,1152]{1,0:T(8,128)(2,1)}, u32[]{:S(2)}) copy-start(bf16[1152,1152]{1,0:T(8,128)(2,1)} %weight.1) | copy-start | bytes 7962628

commit v4 on v3

--- a/solution.py
+++ b/solution.py
@@ -13,6 +13,7 @@
 HEADS = 16
 LANES = 128
 PIECE = 768
+FINISH_PIECE = 512
 SUM_ROWS = 8
 CORE_MASK = 1
 MERGE_MASK = 2
@@ -342,14 +343,27 @@
 
 
 def finish_kernel(
-    value_a, lse_a, expand, packed_b, x_in, row_valid, sums_a, sums_b, weight, out
+    value_a, lse_a, expand, packed_b, x_in, row_valid, sums_a, sums_b, weight, out_far, out, sent
 ):
-    value = merge(value_a[...], lse_a[...], packed_b[...], expand[...])
+    width = out.shape[1]
+    value = merge(value_a[...], lse_a[...], packed_b[...], expand[...]).astype(jnp.bfloat16)
     gate = sum_piece(sums_a[...].astype(jnp.float32) + sums_b[...].astype(jnp.float32), 2)
-    projected = jnp.dot(
-        value.astype(jnp.bfloat16), weight[...], preferred_element_type=jnp.float32
-    )
-    out[...] = (x_in[...] + gate * projected * row_valid[:, 0:1]).astype(jnp.bfloat16)
+    copies = []
+    for index, start in enumerate(range(0, width, FINISH_PIECE)):
+        columns = slice(start, min(start + FINISH_PIECE, width))
+        projected = jnp.dot(value, weight[:, columns], preferred_element_type=jnp.float32)
+        out[:, columns] = (
+            x_in[:, columns] + gate[:, columns] * projected * row_valid[:, 0:1]
+        ).astype(jnp.bfloat16)
+        size = columns.stop - columns.start
+        copies.append(
+            pltpu.make_async_copy(
+                out.at[:, pl.ds(start, size)], out_far.at[:, pl.ds(start, size)], sent.at[index]
+            )
+        )
+        copies[-1].start()
+    for copy in copies:
+        copy.wait()
 
 
 def far():
@@ -471,7 +485,11 @@
         finish_kernel,
         out_shape=shape((rows, width), jnp.bfloat16),
         in_specs=[vmem()] * 9,
-        out_specs=vmem(),
+        out_specs=far(),
+        scratch_shapes=[
+            pltpu.VMEM((rows, width), jnp.bfloat16),
+            pltpu.SemaphoreType.DMA((-(-width // FINISH_PIECE),)),
+        ],
         compiler_params=grant(8),
         name="finish",
     )(

time: 35.6 us -> 35.6 us (level)
  no operation moved by 1% of the time
where the time goes in v4:
time: 35.6 us; the launch traced here: 35.4 us
  starting transfers between devices  15.2 us (43%)
  waiting for transfers between devices  10 us (28%)
  Pallas kernels  9.44 us (27%)
  between operations  0.69 us (2%)
    ppermute x14, starting transfers between devices, swap(): return lax.ppermute(value, 'patch', pairs)  15.2 us
    ppermute x14, waiting for transfers between devices, swap(): return lax.ppermute(value, 'patch', pairs)  10 us
    pallas_call x1, Pallas kernels, per_device(): pl.pallas_call(functools.partial(attend_kernel, rows, len(key_parts)), ou...  4.14 us
    pallas_call x1, Pallas kernels, per_device(): pl.pallas_call(functools.partial(front_kernel, part_index, len(key_masks)...  2.03 us
    pallas_call x1, Pallas kernels, per_device(): pl.pallas_call(own_kernel, out_shape=(shape((rows, width + LANES), jnp.bf...  1.63 us
    pallas_call x1, Pallas kernels, per_device(): pl.pallas_call(finish_kernel, out_shape=shape((rows, width), jnp.bfloat16...  1.55 us
  transfers between devices with their start and end apart: 14, of which 6 were waited for; matrix products, arithmetic and copies ran while one was open for 0% of the time, Pallas kernels for 5%

profile of v4, /device:TPU:0, one launch (start us, length us, event | category | flops | bytes accessed | tf_op | source)
XLA Modules:
  0.0 35.4 jit_solution(16671706200726582319)
XLA Ops:
  0.7 2.0 %front.1 = (bf16[48,1152]{1,0:T(8,128)(2,1)S(1)}, bf16[8,1152]{1,0:T(8,128)(2,1)S(1)}, f32[48,1152]{1,0:T(8,128)S(1)}, f32[8,384]{1,0:T(8,128)S(1)}, f32[48,128]{1,0:T(8,128)S(1)}) custom-call(s32[1]{0:T(128)S(6)} %copy.11.timestep, s32[16]{0:T(128)} %counts_far.1, bf16[48,1152]{1,0:T(8,128)(2,1)} %tokens_far.1, s32[2,48]{1,0:T(2,128)} %positions_far.1, ...), custom_call_target="tpu_custom_call" | custom-call | tf_op jit(solution)/shard_map/front/pallas_call | solution.py:398
  2.7 0.6 %collective-permute-start = (bf16[8,1152]{1,0:T(8,128)(2,1)S(1)}, bf16[8,1152]{1,0:T(8,128)(2,1)S(1)}, u32[]{:S(2)}, u32[]{:S(2)}) collective-permute-start(bf16[8,1152]{1,0:T(8,128)(2,1)S(1)} %get-tuple-element.18.refs_0_), channel_id=1, source_target_pairs={{0,1},{1,0},{2,3},{3,2},{4,5},{5,4},{6,7},{7,6},{8,9},{9,8},{10,11... | collective-permute-start | bytes 55304 | tf_op jit(solution)/shard_map/ppermute | solution.py:390
  3.3 0.8 %collective-permute-done.refs_1_ = bf16[8,1152]{1,0:T(8,128)(2,1)S(1)} collective-permute-done((bf16[8,1152]{1,0:T(8,128)(2,1)S(1)}, bf16[8,1152]{1,0:T(8,128)(2,1)S(1)}, u32[]{:S(2)}, u32[]{:S(2)}) %collective-permute-start) | collective-permute-done | bytes 18464 | tf_op jit(solution)/shard_map/ppermute | solution.py:390
  4.1 5.0 %collective-permute-start.3 = (bf16[8,1152]{1,0:T(8,128)(2,1)S(1)}, bf16[8,1152]{1,0:T(8,128)(2,1)S(1)}, u32[]{:S(2)}, u32[]{:S(2)}) collective-permute-start(bf16[8,1152]{1,0:T(8,128)(2,1)S(1)} %add.2.refs_0_), channel_id=1, source_target_pairs={{0,12},{1,13},{2,14},{3,15},{4,8},{5,9},{6,10},{7,11},{8,4},{9,5},... | collective-permute-start | bytes 55304 | tf_op jit(solution)/shard_map/ppermute | solution.py:390
  9.1 0.0 collective-permute-start.2
  9.1 0.6 %collective-permute-start.1 = (bf16[8,1152]{1,0:T(8,128)(2,1)S(1)}, bf16[8,1152]{1,0:T(8,128)(2,1)S(1)}, u32[]{:S(2)}, u32[]{:S(2)}) collective-permute-start(bf16[8,1152]{1,0:T(8,128)(2,1)S(1)} %add.2.refs_0_), channel_id=1, source_target_pairs={{0,4},{1,5},{2,6},{3,7},{4,0},{5,1},{6,2},{7,3},{8,12},{9,13},{10,... | collective-permute-start | bytes 55304 | tf_op jit(solution)/shard_map/ppermute | solution.py:390
  9.8 3.7 %collective-permute-start.7 = (bf16[48,1152]{1,0:T(8,128)(2,1)S(1)}, bf16[48,1152]{1,0:T(8,128)(2,1)S(1)}, u32[]{:S(2)}, u32[]{:S(2)}) collective-permute-start(bf16[48,1152]{1,0:T(8,128)(2,1)S(1)} %get-tuple-element.19.refs_3_.refs_11_), channel_id=1, source_target_pairs={{0,12},{1,13},{2,14},{3,15},{4,8},{5,9},{6,10},{7,11},{8,4},{9,5},... | collective-permute-start | bytes 331784 | tf_op jit(solution)/shard_map/ppermute | solution.py:390
  13.5 0.0 collective-permute-start.6
  13.5 0.0 collective-permute-done.3.refs_3_
  13.5 0.6 %collective-permute-start.5 = (bf16[48,1152]{1,0:T(8,128)(2,1)S(1)}, bf16[48,1152]{1,0:T(8,128)(2,1)S(1)}, u32[]{:S(2)}, u32[]{:S(2)}) collective-permute-start(bf16[48,1152]{1,0:T(8,128)(2,1)S(1)} %get-tuple-element.19.refs_3_.refs_11_), channel_id=1, source_target_pairs={{0,4},{1,5},{2,6},{3,7},{4,0},{5,1},{6,2},{7,3},{8,12},{9,13},{10,... | collective-permute-start | bytes 331784 | tf_op jit(solution)/shard_map/ppermute | solution.py:390
  14.2 0.0 collective-permute-done.2.refs_2_
  14.2 0.0 collective-permute-done.1.refs_1_
  14.2 1.7 %collective-permute-start.4 = (bf16[8,1152]{1,0:T(8,128)(2,1)S(1)}, bf16[8,1152]{1,0:T(8,128)(2,1)S(1)}, u32[]{:S(2)}, u32[]{:S(2)}) collective-permute-start(bf16[8,1152]{1,0:T(8,128)(2,1)S(1)} %add.3.refs_1_.sums_a), channel_id=1, source_target_pairs={{0,2},{1,3},{2,0},{3,1},{4,6},{5,7},{6,4},{7,5},{8,10},{9,11},{10,... | collective-permute-start | bytes 55304 | tf_op jit(solution)/shard_map/ppermute | solution.py:390
  15.9 0.4 %collective-permute-start.12 = (bf16[48,1152]{1,0:T(8,128)(2,1)S(1)}, bf16[48,1152]{1,0:T(8,128)(2,1)S(1)}, u32[]{:S(2)}, u32[]{:S(2)}) collective-permute-start(bf16[48,1152]{1,0:T(8,128)(2,1)S(1)} %get-tuple-element.19.refs_3_.refs_11_), channel_id=1, source_target_pairs={{0,2},{1,3},{2,0},{3,1},{4,6},{5,7},{6,4},{7,5},{8,10},{9,11},{10,... | collective-permute-start | bytes 331784 | tf_op jit(solution)/shard_map/ppermute | solution.py:390
  16.3 1.9 %collective-permute-done.4.refs_2_.sums_b = bf16[8,1152]{1,0:T(8,128)(2,1)S(1)} collective-permute-done((bf16[8,1152]{1,0:T(8,128)(2,1)S(1)}, bf16[8,1152]{1,0:T(8,128)(2,1)S(1)}, u32[]{:S(2)}, u32[]{:S(2)}) %collective-permute-start.4) | collective-permute-done | bytes 18464 | tf_op jit(solution)/shard_map/ppermute | solution.py:390
  18.2 0.0 collective-permute-start.8
  18.2 0.0 collective-permute-done.7.refs_6_
  18.2 0.5 %collective-permute-start.11 = (bf16[48,1152]{1,0:T(8,128)(2,1)S(1)}, bf16[48,1152]{1,0:T(8,128)(2,1)S(1)}, u32[]{:S(2)}, u32[]{:S(2)}) collective-permute-start(bf16[48,1152]{1,0:T(8,128)(2,1)S(1)} %collective-permute-done.7.refs_6_), channel_id=1, source_target_pairs={{0,1},{1,0},{2,3},{3,2},{4,5},{5,4},{6,7},{7,6},{8,9},{9,8},{10,11... | collective-permute-start | bytes 331784 | tf_op jit(solution)/shard_map/ppermute | solution.py:390
  18.8 3.8 %collective-permute-done.6.refs_5_ = bf16[48,1152]{1,0:T(8,128)(2,1)S(1)} collective-permute-done((bf16[48,1152]{1,0:T(8,128)(2,1)S(1)}, bf16[48,1152]{1,0:T(8,128)(2,1)S(1)}, u32[]{:S(2)}, u32[]{:S(2)}) %collective-permute-start.6) | collective-permute-done | bytes 110624 | tf_op jit(solution)/shard_map/ppermute | solution.py:390
  22.6 0.0 collective-permute-start.10
  22.6 0.0 collective-permute-done.5.refs_4_
  22.6 0.5 %collective-permute-start.9 = (bf16[48,1152]{1,0:T(8,128)(2,1)S(1)}, bf16[48,1152]{1,0:T(8,128)(2,1)S(1)}, u32[]{:S(2)}, u32[]{:S(2)}) collective-permute-start(bf16[48,1152]{1,0:T(8,128)(2,1)S(1)} %collective-permute-done.5.refs_4_), channel_id=1, source_target_pairs={{0,1},{1,0},{2,3},{3,2},{4,5},{5,4},{6,7},{7,6},{8,9},{9,8},{10,11... | collective-permute-start | bytes 331784 | tf_op jit(solution)/shard_map/ppermute | solution.py:390
  23.1 0.0 collective-permute-done.12.refs_12_
  23.1 0.0 collective-permute-done.8.refs_7_
  23.1 0.0 collective-permute-done.11.refs_10_
  23.1 0.8 %collective-permute-done.10.refs_9_ = bf16[48,1152]{1,0:T(8,128)(2,1)S(1)} collective-permute-done((bf16[48,1152]{1,0:T(8,128)(2,1)S(1)}, bf16[48,1152]{1,0:T(8,128)(2,1)S(1)}, u32[]{:S(2)}, u32[]{:S(2)}) %collective-permute-start.10) | collective-permute-done | bytes 110624 | tf_op jit(solution)/shard_map/ppermute | solution.py:390
  23.9 0.2 collective-permute-done.9.refs_8_
  24.1 4.1 %attend.1 = (bf16[48,1152]{1,0:T(8,128)(2,1)S(1)}, bf16[384,1152]{1,0:T(8,128)(2,1)S(1)}, bf16[384,1152]{1,0:T(8,128)(2,1)S(1)}, bf16[48,1280]{1,0:T(8,128)(2,1)S(1)}) custom-call(f32[8,384]{1,0:T(8,128)S(1)} %get-tuple-element.17.refs_0_.bias, bf16[8,1152]{1,0:T(8,128)(2,1)S(1)} %add.3.refs_1_.sums_a, ...), custom_call_target="tpu_custom_call" | custom-call | tf_op jit(solution)/shard_map/attend/pallas_call | solution.py:451
  28.2 1.6 %collective-permute-start.13 = (bf16[48,1280]{1,0:T(8,128)(2,1)S(1)}, bf16[48,1280]{1,0:T(8,128)(2,1)S(1)}, u32[]{:S(2)}, u32[]{:S(2)}) collective-permute-start(bf16[48,1280]{1,0:T(8,128)(2,1)S(1)} %get-tuple-element.26), channel_id=1, source_target_pairs={{0,2},{1,3},{2,0},{3,1},{4,6},{5,7},{6,4},{7,5},{8,10},{9,11},{10,... | collective-permute-start | bytes 368648 | tf_op jit(solution)/shard_map/ppermute | solution.py:390
  29.8 1.6 %own.1 = (bf16[48,1280]{1,0:T(8,128)(2,1)S(1)}, f32[48,128]{1,0:T(8,128)S(1)}, bf16[128,1152]{1,0:T(8,128)(2,1)S(1)}) custom-call(f32[8,384]{1,0:T(8,128)S(1)} %get-tuple-element.17.refs_0_.bias, bf16[48,1152]{1,0:T(8,128)(2,1)S(1)} %get-tuple-element.20.query, bf16[384,1152]{1,0:T(8,128)(2,1)S(1)} %get-tuple-element.21.keys, ...), custom_call_target="tpu_custom_call" | custom-call | flops 17179869184 | bytes 1769472 | tf_op jit(solution)/shard_map/own/pallas_call | solution.py:469
  31.4 2.5 %collective-permute-done.13.packed_b = bf16[48,1280]{1,0:T(8,128)(2,1)S(1)} collective-permute-done((bf16[48,1280]{1,0:T(8,128)(2,1)S(1)}, bf16[48,1280]{1,0:T(8,128)(2,1)S(1)}, u32[]{:S(2)}, u32[]{:S(2)}) %collective-permute-start.13) | collective-permute-done | bytes 122912 | tf_op jit(solution)/shard_map/ppermute | solution.py:390
  33.9 1.5 %finish.1 = bf16[48,1152]{1,0:T(8,128)(2,1)} custom-call(bf16[48,1280]{1,0:T(8,128)(2,1)S(1)} %get-tuple-element.23.value_a, f32[48,128]{1,0:T(8,128)S(1)} %get-tuple-element.24.lse_a, bf16[128,1152]{1,0:T(8,128)(2,1)S(1)} %get-tuple-element.25.expand, bf16[48,1280]{1,0:T(8,128)(2,1)S(1)} %collective-permute-done.13.packed_b, ...), custom_call_target="tpu_custom_call" | custom-call | tf_op jit(solution)/shard_map/finish/pallas_call | solution.py:484
  (9 shorter events, 0.1 us)
Async XLA Ops:
  2.7 1.4 %collective-permute-start = (bf16[8,1152]{1,0:T(8,128)(2,1)S(1)}, bf16[8,1152]{1,0:T(8,128)(2,1)S(1)}, u32[]{:S(2)}, u32[]{:S(2)}) collective-permute-start(bf16[8,1152]{1,0:T(8,128)(2,1)S(1)} %get-tuple-element.18.refs_0_), channel_id=1, source_target_pairs={{0,1},{1,0},{2,3},{3,2},{4,5},{5,4},{6,7},{7,6},{8,9},{9,8},{10,11... | collective-permute-start | bytes 55304 | tf_op jit(solution)/shard_map/ppermute | solution.py:390
  4.1 9.4 %collective-permute-start.3 = (bf16[8,1152]{1,0:T(8,128)(2,1)S(1)}, bf16[8,1152]{1,0:T(8,128)(2,1)S(1)}, u32[]{:S(2)}, u32[]{:S(2)}) collective-permute-start(bf16[8,1152]{1,0:T(8,128)(2,1)S(1)} %add.2.refs_0_), channel_id=1, source_target_pairs={{0,12},{1,13},{2,14},{3,15},{4,8},{5,9},{6,10},{7,11},{8,4},{9,5},... | collective-permute-start | bytes 55304 | tf_op jit(solution)/shard_map/ppermute | solution.py:390
  9.1 5.0 %collective-permute-start.2 = (bf16[8,1152]{1,0:T(8,128)(2,1)S(1)}, bf16[8,1152]{1,0:T(8,128)(2,1)S(1)}, u32[]{:S(2)}, u32[]{:S(2)}) collective-permute-start(bf16[8,1152]{1,0:T(8,128)(2,1)S(1)} %add.2.refs_0_), channel_id=1, source_target_pairs={{0,8},{1,9},{2,10},{3,11},{4,12},{5,13},{6,14},{7,15},{8,0},{9,1},... | collective-permute-start | bytes 55304 | tf_op jit(solution)/shard_map/ppermute | solution.py:390
  9.1 5.0 %collective-permute-start.1 = (bf16[8,1152]{1,0:T(8,128)(2,1)S(1)}, bf16[8,1152]{1,0:T(8,128)(2,1)S(1)}, u32[]{:S(2)}, u32[]{:S(2)}) collective-permute-start(bf16[8,1152]{1,0:T(8,128)(2,1)S(1)} %add.2.refs_0_), channel_id=1, source_target_pairs={{0,4},{1,5},{2,6},{3,7},{4,0},{5,1},{6,2},{7,3},{8,12},{9,13},{10,... | collective-permute-start | bytes 55304 | tf_op jit(solution)/shard_map/ppermute | solution.py:390
  9.8 14.3 %slice-start = ((s8[7962624]{0:T(1024)(128)(4,1)}), s8[4194304]{0:T(1024)(128)(4,1)S(1)}, s32[]{:S(2)}) async-start(s8[7962624]{0:T(1024)(128)(4,1)} %bitcast.1), calls=%async_computation | async-start | bytes 8388608
  9.8 14.3 %slice-start.1 = ((s8[7962624]{0:T(1024)(128)(4,1)}), s8[3768320]{0:T(1024)(128)(4,1)S(1)}, s32[]{:S(2)}) async-start(s8[7962624]{0:T(1024)(128)(4,1)} %bitcast.1), calls=%async_computation.1 | async-start | bytes 7536640
  9.8 8.5 %collective-permute-start.7 = (bf16[48,1152]{1,0:T(8,128)(2,1)S(1)}, bf16[48,1152]{1,0:T(8,128)(2,1)S(1)}, u32[]{:S(2)}, u32[]{:S(2)}) collective-permute-start(bf16[48,1152]{1,0:T(8,128)(2,1)S(1)} %get-tuple-element.19.refs_3_.refs_11_), channel_id=1, source_target_pairs={{0,12},{1,13},{2,14},{3,15},{4,8},{5,9},{6,10},{7,11},{8,4},{9,5},... | collective-permute-start | bytes 331784 | tf_op jit(solution)/shard_map/ppermute | solution.py:390
  13.5 9.1 %collective-permute-start.6 = (bf16[48,1152]{1,0:T(8,128)(2,1)S(1)}, bf16[48,1152]{1,0:T(8,128)(2,1)S(1)}, u32[]{:S(2)}, u32[]{:S(2)}) collective-permute-start(bf16[48,1152]{1,0:T(8,128)(2,1)S(1)} %get-tuple-element.19.refs_3_.refs_11_), channel_id=1, source_target_pairs={{0,8},{1,9},{2,10},{3,11},{4,12},{5,13},{6,14},{7,15},{8,0},{9,1},... | collective-permute-start | bytes 331784 | tf_op jit(solution)/shard_map/ppermute | solution.py:390
  13.5 9.1 %collective-permute-start.5 = (bf16[48,1152]{1,0:T(8,128)(2,1)S(1)}, bf16[48,1152]{1,0:T(8,128)(2,1)S(1)}, u32[]{:S(2)}, u32[]{:S(2)}) collective-permute-start(bf16[48,1152]{1,0:T(8,128)(2,1)S(1)} %get-tuple-element.19.refs_3_.refs_11_), channel_id=1, source_target_pairs={{0,4},{1,5},{2,6},{3,7},{4,0},{5,1},{6,2},{7,3},{8,12},{9,13},{10,... | collective-permute-start | bytes 331784 | tf_op jit(solution)/shard_map/ppermute | solution.py:390
  14.2 4.0 %collective-permute-start.4 = (bf16[8,1152]{1,0:T(8,128)(2,1)S(1)}, bf16[8,1152]{1,0:T(8,128)(2,1)S(1)}, u32[]{:S(2)}, u32[]{:S(2)}) collective-permute-start(bf16[8,1152]{1,0:T(8,128)(2,1)S(1)} %add.3.refs_1_.sums_a), channel_id=1, source_target_pairs={{0,2},{1,3},{2,0},{3,1},{4,6},{5,7},{6,4},{7,5},{8,10},{9,11},{10,... | collective-permute-start | bytes 55304 | tf_op jit(solution)/shard_map/ppermute | solution.py:390
  15.9 7.2 %collective-permute-start.12 = (bf16[48,1152]{1,0:T(8,128)(2,1)S(1)}, bf16[48,1152]{1,0:T(8,128)(2,1)S(1)}, u32[]{:S(2)}, u32[]{:S(2)}) collective-permute-start(bf16[48,1152]{1,0:T(8,128)(2,1)S(1)} %get-tuple-element.19.refs_3_.refs_11_), channel_id=1, source_target_pairs={{0,2},{1,3},{2,0},{3,1},{4,6},{5,7},{6,4},{7,5},{8,10},{9,11},{10,... | collective-permute-start | bytes 331784 | tf_op jit(solution)/shard_map/ppermute | solution.py:390
  18.2 4.9 %collective-permute-start.8 = (bf16[48,1152]{1,0:T(8,128)(2,1)S(1)}, bf16[48,1152]{1,0:T(8,128)(2,1)S(1)}, u32[]{:S(2)}, u32[]{:S(2)}) collective-permute-start(bf16[48,1152]{1,0:T(8,128)(2,1)S(1)} %get-tuple-element.19.refs_3_.refs_11_), channel_id=1, source_target_pairs={{0,1},{1,0},{2,3},{3,2},{4,5},{5,4},{6,7},{7,6},{8,9},{9,8},{10,11... | collective-permute-start | bytes 331784 | tf_op jit(solution)/shard_map/ppermute | solution.py:390
  18.2 4.9 %collective-permute-start.11 = (bf16[48,1152]{1,0:T(8,128)(2,1)S(1)}, bf16[48,1152]{1,0:T(8,128)(2,1)S(1)}, u32[]{:S(2)}, u32[]{:S(2)}) collective-permute-start(bf16[48,1152]{1,0:T(8,128)(2,1)S(1)} %collective-permute-done.7.refs_6_), channel_id=1, source_target_pairs={{0,1},{1,0},{2,3},{3,2},{4,5},{5,4},{6,7},{7,6},{8,9},{9,8},{10,11... | collective-permute-start | bytes 331784 | tf_op jit(solution)/shard_map/ppermute | solution.py:390
  22.6 1.3 %collective-permute-start.10 = (bf16[48,1152]{1,0:T(8,128)(2,1)S(1)}, bf16[48,1152]{1,0:T(8,128)(2,1)S(1)}, u32[]{:S(2)}, u32[]{:S(2)}) collective-permute-start(bf16[48,1152]{1,0:T(8,128)(2,1)S(1)} %collective-permute-done.6.refs_5_), channel_id=1, source_target_pairs={{0,1},{1,0},{2,3},{3,2},{4,5},{5,4},{6,7},{7,6},{8,9},{9,8},{10,11... | collective-permute-start | bytes 331784 | tf_op jit(solution)/shard_map/ppermute | solution.py:390
  22.6 1.5 %collective-permute-start.9 = (bf16[48,1152]{1,0:T(8,128)(2,1)S(1)}, bf16[48,1152]{1,0:T(8,128)(2,1)S(1)}, u32[]{:S(2)}, u32[]{:S(2)}) collective-permute-start(bf16[48,1152]{1,0:T(8,128)(2,1)S(1)} %collective-permute-done.5.refs_4_), channel_id=1, source_target_pairs={{0,1},{1,0},{2,3},{3,2},{4,5},{5,4},{6,7},{7,6},{8,9},{9,8},{10,11... | collective-permute-start | bytes 331784 | tf_op jit(solution)/shard_map/ppermute | solution.py:390
  28.2 5.6 %collective-permute-start.13 = (bf16[48,1280]{1,0:T(8,128)(2,1)S(1)}, bf16[48,1280]{1,0:T(8,128)(2,1)S(1)}, u32[]{:S(2)}, u32[]{:S(2)}) collective-permute-start(bf16[48,1280]{1,0:T(8,128)(2,1)S(1)} %get-tuple-element.26), channel_id=1, source_target_pairs={{0,2},{1,3},{2,0},{3,1},{4,6},{5,7},{6,4},{7,5},{8,10},{9,11},{10,... | collective-permute-start | bytes 368648 | tf_op jit(solution)/shard_map/ppermute | solution.py:390
  29.8 4.1 %copy-start = (bf16[1152,1152]{1,0:T(8,128)(2,1)S(1)}, bf16[1152,1152]{1,0:T(8,128)(2,1)}, u32[]{:S(2)}) copy-start(bf16[1152,1152]{1,0:T(8,128)(2,1)} %weight.1) | copy-start | bytes 7962628
